TPU v7x, 512 devices: a 4x2x32 block of a 4x8x32 slice. The times are simulated.
512 devices in a mesh: group: 2 (over y), seq: 128 (over x, z), head: 2 (over core).
Axes of the slice: x: 4, y: 2, z: 32, core: 2. Of those that a mesh axis runs over, the one named last changes fastest.
The devices are a block of a 4x8x32 slice.
Arguments:
- queries: bfloat16 [32768, 3, 2560], P(('group', 'seq'), None, 'head'), parts along dimension 0, may hold values from -6 to 6, as said below
- keys: bfloat16 [32768, 512], P(('group', 'seq'), 'head'), parts along dimension 0, may hold values from -6 to 6, as said below
- values: bfloat16 [32768, 512], P(('group', 'seq'), 'head'), parts along dimension 0, may hold values from -6 to 6
- lengths: int32 [128], P('group'), parts along dimension 0, may hold values from 1 to 1024, 16384 in all
- page_owner: int32 [8192, 4], P(('group', 'seq'), 'head'), parts along dimension 0, may hold values from 0 to 127, as said below
- page_slot: int32 [8192, 4], P(('group', 'seq'), 'head'), parts along dimension 0, may hold values from 0 to 63, as said below
Outputs:
- attended: bfloat16 [32768, 3, 2560], P(('group', 'seq'), None, 'head'), parts along dimension 0
- cache_pages: bfloat16 [32768, 4, 256], P(('group', 'seq', 'head')), parts along dimension 0
There are 2 independent parts, one for each index of `group`. A program takes and returns all parts, laid end to end along the dimension named above; each array names one. Nothing has to cross between parts.
Inputs may be any that keep to these rules, and one draw needn't show every extreme that they name: `page_owner`: for each index g of the head axis, the pages of KV heads g * 2 to g * 2 + 1 held by one index of seq include at most one page for any one owner, and that bound is reached; every owner receives exactly 64 such pages. `page_slot`: the pages that one owner receives for one index of the head axis have distinct slots. `queries`: entries lie within the range; they are of order one. `keys`: entries lie within the range; they are of order one. `lengths`: sum to 16384; the largest is exactly 1024.
All inputs are finite; a program needn't handle non-finite values.
Results may differ from a plain program's by a relative error of at most 0.0029.
Values may be sent and summed in bfloat16 or wider, within the bound.
A program may use at most 64 MiB of HBM per device.

v0:
```python
import math

import jax
import jax.numpy as jnp
from jax import lax
from jax.sharding import PartitionSpec as P

LAYERS = 3
QPER = 5
HD = 128
PAGE = 4


negative_fill = -1e30


def shifted(x, axis, by):
    count = lax.axis_size(axis)
    pairs = [(i, i + by) for i in range(count) if 0 <= i + by < count]
    return lax.ppermute(x, axis, pairs)


def request_ids(positions, starts):
    return jnp.sum((starts[None, :] <= positions[:, None]).astype(jnp.int32), axis=1) - 1


def shards(queries, keys, values, lengths, page_owner, page_slot):
    tok_rows = keys.shape[0]
    kv_local = keys.shape[1] // HD
    seq_count = lax.axis_size("seq")
    reach = min(8, seq_count // 2)
    mine = lax.axis_index("seq")
    starts = jnp.cumsum(lengths) - lengths
    local_iota = jnp.arange(tok_rows, dtype=jnp.int32)
    query_pos = mine * tok_rows + local_iota
    query_req = request_ids(query_pos, starts)
    grouped = queries.reshape(tok_rows, LAYERS, kv_local, QPER, HD)
    scale = 1.0 / math.sqrt(HD)

    def attend(carry, block, anchor):
        key_pos = anchor * tok_rows + local_iota
        key_req = request_ids(key_pos, starts)
        allowed = (
            (query_req[:, None] == key_req[None, :])
            & (key_pos[None, :] <= query_pos[:, None])
            & (key_pos[None, :] >= 0)
        )
        maxima, totals, summed = carry
        block_keys = block[0].reshape(tok_rows, kv_local, HD)
        block_vals = block[1].reshape(tok_rows, kv_local, HD)
        scores = (
            jnp.einsum("tlcqd,kcd->tlcqk", grouped, block_keys, preferred_element_type=jnp.float32)
            * scale
        )
        wide = allowed[:, None, None, None, :]
        masked = jnp.where(wide, scores, negative_fill)
        fresh = jnp.maximum(maxima, jnp.max(masked, axis=-1))
        shrink = jnp.exp(maxima - fresh)
        weights = jnp.where(wide, jnp.exp(masked - fresh[..., None]), 0.0)
        totals = totals * shrink + jnp.sum(weights, axis=-1)
        product = jnp.einsum(
            "tlcqk,kcd->tlcqd",
            weights.astype(jnp.bfloat16),
            block_vals,
            preferred_element_type=jnp.float32,
        )
        summed = summed * shrink[..., None] + product
        return (fresh, totals, summed)

    stat_shape = (tok_rows, LAYERS, kv_local, QPER)
    carry = (
        jnp.full(stat_shape, negative_fill, jnp.float32),
        jnp.zeros(stat_shape, jnp.float32),
        jnp.zeros(stat_shape + (HD,), jnp.float32),
    )
    pair = jnp.stack([keys, values])
    carry = attend(carry, pair, mine)
    moving = pair
    for step in range(1, reach + 1):
        moving = shifted(moving, "seq", 1)
        carry = attend(carry, moving, mine - step)
    maxima, totals, summed = carry
    attended = (
        (summed / totals[..., None])
        .astype(jnp.bfloat16)
        .reshape(tok_rows, LAYERS, kv_local * QPER * HD)
    )
    pages_dev = tok_rows // PAGE
    slots = pages_dev * kv_local
    capacity = max(1, slots // seq_count)
    key_pages = keys.reshape(pages_dev, PAGE, kv_local, HD)
    val_pages = values.reshape(pages_dev, PAGE, kv_local, HD)
    flat_pages = (
        jnp.concatenate([key_pages, val_pages], axis=3)
        .transpose(0, 2, 1, 3)
        .reshape(slots, PAGE * 2 * HD)
    )
    owner = page_owner.reshape(slots)
    slot = page_slot.reshape(slots)
    number = jnp.arange(slots, dtype=jnp.int32)
    earlier = (owner[None, :] == owner[:, None]) & (number[None, :] < number[:, None])
    rank = jnp.sum(earlier.astype(jnp.int32), axis=1)
    target = owner * capacity + rank
    lanes = jnp.arange(seq_count * capacity, dtype=jnp.int32)
    picker = (lanes[:, None] == target[None, :]).astype(jnp.bfloat16)
    outgoing = jnp.dot(picker, flat_pages, preferred_element_type=jnp.float32).astype(jnp.bfloat16)
    outgoing = outgoing.reshape(seq_count, capacity, PAGE * 2 * HD)
    tags = jnp.dot(
        picker, (slot + 1).astype(jnp.bfloat16), preferred_element_type=jnp.float32
    ).astype(jnp.bfloat16)
    tags = tags.reshape(seq_count, capacity)
    received, got_tags = (
        lax.all_to_all(outgoing, "seq", split_axis=0, concat_axis=0, tiled=True),
        lax.all_to_all(tags, "seq", split_axis=0, concat_axis=0, tiled=True),
    )
    received = received.reshape(seq_count * capacity, PAGE * 2 * HD)
    got_tags = got_tags.reshape(seq_count * capacity).astype(jnp.float32)
    placer = (got_tags[None, :] == (number + 1).astype(jnp.float32)[:, None]).astype(jnp.bfloat16)
    cache_pages = jnp.dot(placer, received, preferred_element_type=jnp.float32).astype(jnp.bfloat16)
    cache_pages = cache_pages.reshape(slots, PAGE, 2 * HD)
    return (attended, cache_pages)


def solution(mesh):
    placed = (
        P(("group", "seq"), None, "head"),
        P(("group", "seq"), "head"),
        P(("group", "seq"), "head"),
        P("group"),
        P(("group", "seq"), "head"),
        P(("group", "seq"), "head"),
    )
    return jax.shard_map(
        shards,
        mesh=mesh,
        in_specs=placed,
        out_specs=(P(("group", "seq"), None, "head"), P(("group", "seq", "head"), None, None)),
        check_vma=False,
    )
```

profile of v0, /device:TPU:38, one launch (start us, length us, event | category | flops | bytes accessed | tf_op | source)
XLA Modules:
  0.0 194.5 jit_solution(1295852395093464614)
XLA Ops:
  3.6 52.3 %all-to-all-start = ((bf16[128,1,1]{2,1,0:T(2,128)(2,1)}), bf16[128,1,1]{2,1,0:T(2,128)(2,1)}, u32[]{:S(2)}, u32[]{:S(2)}) async-start(bf16[128,1,1]{2,1,0:T(2,128)(2,1)} %copy.192), calls=%async_computation | async-start | bytes 131072 | tf_op jit(solution)/shard_map/all_to_all | solution.py:114
  55.9 1.0 copy.236
  56.8 1.0 copy.163
  58.5 3.4 %collective-permute-start = (bf16[2,128,256]{1,2,0:T(8,128)(2,1)}, bf16[2,128,256]{1,2,0:T(8,128)(2,1)}, u32[]{:S(2)}, u32[]{:S(2)}) collective-permute-start(bf16[2,128,256]{1,2,0:T(8,128)(2,1)} %pad_maximum_fusion), channel_id=1, source_target_pairs={{0,2},{2,4},{4,6},{6,8},{8,10},{10,12},{12,14},{14,16},{16,18},{18... | collective-permute-start | bytes 393224 | tf_op jit(solution)/shard_map/ppermute | solution.py:20
  62.1 0.9 reshape.1025
  63.0 0.9 reshape_squeeze_stack.6
  63.8 0.9 reshape.1024
  67.5 1.1 and_and_fusion.8
  68.7 1.0 fusion.10
  71.7 0.8 reduce.3
  72.6 0.9 reshape.1054
  73.4 5.3 %all-to-all-done = bf16[128,1,1]{2,1,0:T(2,128)(2,1)} async-done(((bf16[128,1,1]{2,1,0:T(2,128)(2,1)}), bf16[128,1,1]{2,1,0:T(2,128)(2,1)}, u32[]{:S(2)}, u32[]{:S(2)}) %all-to-all-start) | async-done | bytes 288 | tf_op jit(solution)/shard_map/all_to_all | solution.py:114
  78.7 22.7 %all-to-all-start.1 = ((bf16[128,2,512]{2,1,0:T(2,128)(2,1)}), bf16[128,2,512]{2,1,0:T(2,128)(2,1)S(1)}, u32[]{:S(2)}, u32[]{:S(2)}) async-start(bf16[128,2,512]{2,1,0:T(2,128)(2,1)} %reshape.1054), calls=%async_computation.1 | async-start | bytes 524288 | tf_op jit(solution)/shard_map/all_to_all | solution.py:113
  101.4 1.9 convert_reduce_fusion
  103.3 0.9 fusion.160
  104.2 3.4 %collective-permute-start.1 = (bf16[2,128,256]{1,2,0:T(8,128)(2,1)}, bf16[2,128,256]{1,2,0:T(8,128)(2,1)S(1)}, u32[]{:S(2)}, u32[]{:S(2)}) collective-permute-start(bf16[2,128,256]{1,2,0:T(8,128)(2,1)} %collective-permute-done), channel_id=1, source_target_pairs={{0,2},{2,4},{4,6},{6,8},{8,10},{10,12},{12,14},{14,16},{16,18},{18... | collective-permute-start | bytes 393224 | tf_op jit(solution)/shard_map/ppermute | solution.py:20
  107.6 1.2 fusion.11
  108.8 16.5 %collective-permute-done.1 = bf16[2,128,256]{1,2,0:T(8,128)(2,1)S(1)} collective-permute-done((bf16[2,128,256]{1,2,0:T(8,128)(2,1)}, bf16[2,128,256]{1,2,0:T(8,128)(2,1)S(1)}, u32[]{:S(2)}, u32[]{:S(2)}) %collective-permute-start.1) | collective-permute-done | bytes 131104 | tf_op jit(solution)/shard_map/ppermute | solution.py:20
  125.3 2.0 %collective-permute-start.2 = (bf16[2,128,256]{1,2,0:T(8,128)(2,1)S(1)}, bf16[2,128,256]{1,2,0:T(8,128)(2,1)S(1)}, u32[]{:S(2)}, u32[]{:S(2)}) collective-permute-start(bf16[2,128,256]{1,2,0:T(8,128)(2,1)S(1)} %collective-permute-done.1), channel_id=1, source_target_pairs={{0,2},{2,4},{4,6},{6,8},{8,10},{10,12},{12,14},{14,16},{16,18},{18... | collective-permute-start | bytes 393224 | tf_op jit(solution)/shard_map/ppermute | solution.py:20
  127.8 6.6 %collective-permute-done.2 = bf16[2,128,256]{1,2,0:T(8,128)(2,1)S(1)} collective-permute-done((bf16[2,128,256]{1,2,0:T(8,128)(2,1)S(1)}, bf16[2,128,256]{1,2,0:T(8,128)(2,1)S(1)}, u32[]{:S(2)}, u32[]{:S(2)}) %collective-permute-start.2) | collective-permute-done | bytes 131104 | tf_op jit(solution)/shard_map/ppermute | solution.py:20
  134.4 2.1 %collective-permute-start.3 = (bf16[2,128,256]{1,2,0:T(8,128)(2,1)S(1)}, bf16[2,128,256]{1,2,0:T(8,128)(2,1)S(1)}, u32[]{:S(2)}, u32[]{:S(2)}) collective-permute-start(bf16[2,128,256]{1,2,0:T(8,128)(2,1)S(1)} %collective-permute-done.2), channel_id=1, source_target_pairs={{0,2},{2,4},{4,6},{6,8},{8,10},{10,12},{12,14},{14,16},{16,18},{18... | collective-permute-start | bytes 393224 | tf_op jit(solution)/shard_map/ppermute | solution.py:20
  137.1 6.3 %collective-permute-done.3 = bf16[2,128,256]{1,2,0:T(8,128)(2,1)S(1)} collective-permute-done((bf16[2,128,256]{1,2,0:T(8,128)(2,1)S(1)}, bf16[2,128,256]{1,2,0:T(8,128)(2,1)S(1)}, u32[]{:S(2)}, u32[]{:S(2)}) %collective-permute-start.3) | collective-permute-done | bytes 131104 | tf_op jit(solution)/shard_map/ppermute | solution.py:20
  143.4 2.0 %collective-permute-start.4 = (bf16[2,128,256]{1,2,0:T(8,128)(2,1)S(1)}, bf16[2,128,256]{1,2,0:T(8,128)(2,1)S(1)}, u32[]{:S(2)}, u32[]{:S(2)}) collective-permute-start(bf16[2,128,256]{1,2,0:T(8,128)(2,1)S(1)} %collective-permute-done.3), channel_id=1, source_target_pairs={{0,2},{2,4},{4,6},{6,8},{8,10},{10,12},{12,14},{14,16},{16,18},{18... | collective-permute-start | bytes 393224 | tf_op jit(solution)/shard_map/ppermute | solution.py:20
  145.9 6.5 %collective-permute-done.4 = bf16[2,128,256]{1,2,0:T(8,128)(2,1)S(1)} collective-permute-done((bf16[2,128,256]{1,2,0:T(8,128)(2,1)S(1)}, bf16[2,128,256]{1,2,0:T(8,128)(2,1)S(1)}, u32[]{:S(2)}, u32[]{:S(2)}) %collective-permute-start.4) | collective-permute-done | bytes 131104 | tf_op jit(solution)/shard_map/ppermute | solution.py:20
  152.4 2.0 %collective-permute-start.5 = (bf16[2,128,256]{1,2,0:T(8,128)(2,1)S(1)}, bf16[2,128,256]{1,2,0:T(8,128)(2,1)S(1)}, u32[]{:S(2)}, u32[]{:S(2)}) collective-permute-start(bf16[2,128,256]{1,2,0:T(8,128)(2,1)S(1)} %collective-permute-done.4), channel_id=1, source_target_pairs={{0,2},{2,4},{4,6},{6,8},{8,10},{10,12},{12,14},{14,16},{16,18},{18... | collective-permute-start | bytes 393224 | tf_op jit(solution)/shard_map/ppermute | solution.py:20
  154.9 6.5 %collective-permute-done.5 = bf16[2,128,256]{1,2,0:T(8,128)(2,1)S(1)} collective-permute-done((bf16[2,128,256]{1,2,0:T(8,128)(2,1)S(1)}, bf16[2,128,256]{1,2,0:T(8,128)(2,1)S(1)}, u32[]{:S(2)}, u32[]{:S(2)}) %collective-permute-start.5) | collective-permute-done | bytes 131104 | tf_op jit(solution)/shard_map/ppermute | solution.py:20
  161.5 2.0 %collective-permute-start.6 = (bf16[2,128,256]{1,2,0:T(8,128)(2,1)S(1)}, bf16[2,128,256]{1,2,0:T(8,128)(2,1)S(1)}, u32[]{:S(2)}, u32[]{:S(2)}) collective-permute-start(bf16[2,128,256]{1,2,0:T(8,128)(2,1)S(1)} %collective-permute-done.5), channel_id=1, source_target_pairs={{0,2},{2,4},{4,6},{6,8},{8,10},{10,12},{12,14},{14,16},{16,18},{18... | collective-permute-start | bytes 393224 | tf_op jit(solution)/shard_map/ppermute | solution.py:20
  163.9 6.9 %collective-permute-done.6 = bf16[2,128,256]{1,2,0:T(8,128)(2,1)S(1)} collective-permute-done((bf16[2,128,256]{1,2,0:T(8,128)(2,1)S(1)}, bf16[2,128,256]{1,2,0:T(8,128)(2,1)S(1)}, u32[]{:S(2)}, u32[]{:S(2)}) %collective-permute-start.6) | collective-permute-done | bytes 131104 | tf_op jit(solution)/shard_map/ppermute | solution.py:20
  170.8 2.0 %collective-permute-start.7 = (bf16[2,128,256]{1,2,0:T(8,128)(2,1)S(1)}, bf16[2,128,256]{1,2,0:T(8,128)(2,1)S(1)}, u32[]{:S(2)}, u32[]{:S(2)}) collective-permute-start(bf16[2,128,256]{1,2,0:T(8,128)(2,1)S(1)} %collective-permute-done.6), channel_id=1, source_target_pairs={{0,2},{2,4},{4,6},{6,8},{8,10},{10,12},{12,14},{14,16},{16,18},{18... | collective-permute-start | bytes 393224 | tf_op jit(solution)/shard_map/ppermute | solution.py:20
  173.3 6.5 %collective-permute-done.7 = bf16[2,128,256]{1,2,0:T(8,128)(2,1)S(1)} collective-permute-done((bf16[2,128,256]{1,2,0:T(8,128)(2,1)S(1)}, bf16[2,128,256]{1,2,0:T(8,128)(2,1)S(1)}, u32[]{:S(2)}, u32[]{:S(2)}) %collective-permute-start.7) | collective-permute-done | bytes 131104 | tf_op jit(solution)/shard_map/ppermute | solution.py:20
  190.0 1.9 fusion.1
  192.0 1.3 copy.196
  (106 shorter events, 22.8 us)
Async XLA Ops:
  0.6 66.2 %copy-start = (bf16[128,3,1280]{2,0,1:T(8,128)(2,1)S(1)}, bf16[128,3,1280]{2,0,1:T(8,128)(2,1)}, u32[]{:S(2)}) copy-start(bf16[128,3,1280]{2,0,1:T(8,128)(2,1)} %param.6) | copy-start | bytes 2949124
  3.6 75.1 %all-to-all-start = ((bf16[128,1,1]{2,1,0:T(2,128)(2,1)}), bf16[128,1,1]{2,1,0:T(2,128)(2,1)}, u32[]{:S(2)}, u32[]{:S(2)}) async-start(bf16[128,1,1]{2,1,0:T(2,128)(2,1)} %copy.192), calls=%async_computation | async-start | bytes 131072 | tf_op jit(solution)/shard_map/all_to_all | solution.py:114
  58.5 44.8 %collective-permute-start = (bf16[2,128,256]{1,2,0:T(8,128)(2,1)}, bf16[2,128,256]{1,2,0:T(8,128)(2,1)}, u32[]{:S(2)}, u32[]{:S(2)}) collective-permute-start(bf16[2,128,256]{1,2,0:T(8,128)(2,1)} %pad_maximum_fusion), channel_id=1, source_target_pairs={{0,2},{2,4},{4,6},{6,8},{8,10},{10,12},{12,14},{14,16},{16,18},{18... | collective-permute-start | bytes 393224 | tf_op jit(solution)/shard_map/ppermute | solution.py:20
  68.7 1.0 copy-start.8
  73.4 53.9 %copy-start.2 = (pred[128,128]{0,1:T(8,128)(4,1)S(1)}, pred[128,128]{0,1:T(8,128)(4,1)}, u32[]{:S(2)}) copy-start(pred[128,128]{0,1:T(8,128)(4,1)} %get-tuple-element.62) | copy-start | bytes 49156
  78.7 114.5 %all-to-all-start.1 = ((bf16[128,2,512]{2,1,0:T(2,128)(2,1)}), bf16[128,2,512]{2,1,0:T(2,128)(2,1)S(1)}, u32[]{:S(2)}, u32[]{:S(2)}) async-start(bf16[128,2,512]{2,1,0:T(2,128)(2,1)} %reshape.1054), calls=%async_computation.1 | async-start | bytes 524288 | tf_op jit(solution)/shard_map/all_to_all | solution.py:113
  104.2 21.1 %collective-permute-start.1 = (bf16[2,128,256]{1,2,0:T(8,128)(2,1)}, bf16[2,128,256]{1,2,0:T(8,128)(2,1)S(1)}, u32[]{:S(2)}, u32[]{:S(2)}) collective-permute-start(bf16[2,128,256]{1,2,0:T(8,128)(2,1)} %collective-permute-done), channel_id=1, source_target_pairs={{0,2},{2,4},{4,6},{6,8},{8,10},{10,12},{12,14},{14,16},{16,18},{18... | collective-permute-start | bytes 393224 | tf_op jit(solution)/shard_map/ppermute | solution.py:20
  108.8 27.7 %copy-start.3 = (pred[128,128]{0,1:T(8,128)(4,1)S(1)}, pred[128,128]{0,1:T(8,128)(4,1)}, u32[]{:S(2)}) copy-start(pred[128,128]{0,1:T(8,128)(4,1)} %get-tuple-element.55) | copy-start | bytes 49156
  125.3 9.1 %collective-permute-start.2 = (bf16[2,128,256]{1,2,0:T(8,128)(2,1)S(1)}, bf16[2,128,256]{1,2,0:T(8,128)(2,1)S(1)}, u32[]{:S(2)}, u32[]{:S(2)}) collective-permute-start(bf16[2,128,256]{1,2,0:T(8,128)(2,1)S(1)} %collective-permute-done.1), channel_id=1, source_target_pairs={{0,2},{2,4},{4,6},{6,8},{8,10},{10,12},{12,14},{14,16},{16,18},{18... | collective-permute-start | bytes 393224 | tf_op jit(solution)/shard_map/ppermute | solution.py:20
  127.8 17.6 %copy-start.4 = (pred[128,128]{0,1:T(8,128)(4,1)S(1)}, pred[128,128]{0,1:T(8,128)(4,1)}, u32[]{:S(2)}) copy-start(pred[128,128]{0,1:T(8,128)(4,1)} %get-tuple-element.56) | copy-start | bytes 49156
  134.4 9.0 %collective-permute-start.3 = (bf16[2,128,256]{1,2,0:T(8,128)(2,1)S(1)}, bf16[2,128,256]{1,2,0:T(8,128)(2,1)S(1)}, u32[]{:S(2)}, u32[]{:S(2)}) collective-permute-start(bf16[2,128,256]{1,2,0:T(8,128)(2,1)S(1)} %collective-permute-done.2), channel_id=1, source_target_pairs={{0,2},{2,4},{4,6},{6,8},{8,10},{10,12},{12,14},{14,16},{16,18},{18... | collective-permute-start | bytes 393224 | tf_op jit(solution)/shard_map/ppermute | solution.py:20
  137.1 17.3 %copy-start.5 = (pred[128,128]{0,1:T(8,128)(4,1)S(1)}, pred[128,128]{0,1:T(8,128)(4,1)}, u32[]{:S(2)}) copy-start(pred[128,128]{0,1:T(8,128)(4,1)} %get-tuple-element.57) | copy-start | bytes 49156
  143.4 9.0 %collective-permute-start.4 = (bf16[2,128,256]{1,2,0:T(8,128)(2,1)S(1)}, bf16[2,128,256]{1,2,0:T(8,128)(2,1)S(1)}, u32[]{:S(2)}, u32[]{:S(2)}) collective-permute-start(bf16[2,128,256]{1,2,0:T(8,128)(2,1)S(1)} %collective-permute-done.3), channel_id=1, source_target_pairs={{0,2},{2,4},{4,6},{6,8},{8,10},{10,12},{12,14},{14,16},{16,18},{18... | collective-permute-start | bytes 393224 | tf_op jit(solution)/shard_map/ppermute | solution.py:20
  145.9 17.5 %copy-start.6 = (pred[128,128]{0,1:T(8,128)(4,1)S(1)}, pred[128,128]{0,1:T(8,128)(4,1)}, u32[]{:S(2)}) copy-start(pred[128,128]{0,1:T(8,128)(4,1)} %get-tuple-element.58) | copy-start | bytes 49156
  152.4 9.0 %collective-permute-start.5 = (bf16[2,128,256]{1,2,0:T(8,128)(2,1)S(1)}, bf16[2,128,256]{1,2,0:T(8,128)(2,1)S(1)}, u32[]{:S(2)}, u32[]{:S(2)}) collective-permute-start(bf16[2,128,256]{1,2,0:T(8,128)(2,1)S(1)} %collective-permute-done.4), channel_id=1, source_target_pairs={{0,2},{2,4},{4,6},{6,8},{8,10},{10,12},{12,14},{14,16},{16,18},{18... | collective-permute-start | bytes 393224 | tf_op jit(solution)/shard_map/ppermute | solution.py:20
  154.9 17.8 %copy-start.7 = (pred[128,128]{0,1:T(8,128)(4,1)S(1)}, pred[128,128]{0,1:T(8,128)(4,1)}, u32[]{:S(2)}) copy-start(pred[128,128]{0,1:T(8,128)(4,1)} %get-tuple-element.59) | copy-start | bytes 49156
  161.5 9.3 %collective-permute-start.6 = (bf16[2,128,256]{1,2,0:T(8,128)(2,1)S(1)}, bf16[2,128,256]{1,2,0:T(8,128)(2,1)S(1)}, u32[]{:S(2)}, u32[]{:S(2)}) collective-permute-start(bf16[2,128,256]{1,2,0:T(8,128)(2,1)S(1)} %collective-permute-done.5), channel_id=1, source_target_pairs={{0,2},{2,4},{4,6},{6,8},{8,10},{10,12},{12,14},{14,16},{16,18},{18... | collective-permute-start | bytes 393224 | tf_op jit(solution)/shard_map/ppermute | solution.py:20
  170.8 9.0 %collective-permute-start.7 = (bf16[2,128,256]{1,2,0:T(8,128)(2,1)S(1)}, bf16[2,128,256]{1,2,0:T(8,128)(2,1)S(1)}, u32[]{:S(2)}, u32[]{:S(2)}) collective-permute-start(bf16[2,128,256]{1,2,0:T(8,128)(2,1)S(1)} %collective-permute-done.6), channel_id=1, source_target_pairs={{0,2},{2,4},{4,6},{6,8},{8,10},{10,12},{12,14},{14,16},{16,18},{18... | collective-permute-start | bytes 393224 | tf_op jit(solution)/shard_map/ppermute | solution.py:20
  173.2 7.0 %copy-start.10 = (f32[128,3,2,5]{0,3,1,2:T(8,128)S(1)}, f32[128,3,2,5]{0,3,1,2:T(8,128)}, u32[]{:S(2)}) copy-start(f32[128,3,2,5]{0,3,1,2:T(8,128)} %get-tuple-element.79) | copy-start | bytes 46084
  173.2 7.1 %copy-start.9 = (pred[128,128]{0,1:T(8,128)(4,1)S(1)}, pred[128,128]{0,1:T(8,128)(4,1)}, u32[]{:S(2)}) copy-start(pred[128,128]{0,1:T(8,128)(4,1)} %copy-done.8) | copy-start | bytes 49156
  186.5 1.1 copy-start.1
  191.9 1.6 copy-start.11
where the time goes:
time: 195 us; the launch traced here: 194 us
  starting transfers between devices  93.7 us (48%)
  waiting for transfers between devices  61.2 us (31%)
  matrix products  12.9 us (7%)
  other arithmetic  12.8 us (7%)
  local copies, waits for them, and re-layouts  12.6 us (6%)
    ppermute x8, waiting for transfers between devices, shifted(): return lax.ppermute(x, axis, pairs)  55.8 us
    all_to_all x1, starting transfers between devices, shards(): lax.all_to_all(tags, 'seq', split_axis=0, concat_axis=0, tiled=True)  52.3 us
    all_to_all x1, starting transfers between devices, shards(): lax.all_to_all(outgoing, 'seq', split_axis=0, concat_axis=0, tiled=True)  22.7 us
    ppermute x8, starting transfers between devices, shifted(): return lax.ppermute(x, axis, pairs)  18.7 us
    dot_general x9, matrix products, attend(): jnp.einsum('tlcqk,kcd->tlcqd', weights.astype(jnp.bfloat16), block_vals,...  6.68 us
    dot_general x9, matrix products, attend(): jnp.einsum('tlcqd,kcd->tlcqk', grouped, block_keys, preferred_element_typ...  5.62 us
    all_to_all x1, waiting for transfers between devices, shards(): lax.all_to_all(tags, 'seq', split_axis=0, concat_axis=0, tiled=True)  5.31 us
    unnamed x31, local copies, waits for them, and re-layouts  4.84 us
  transfers between devices with their start and end apart: 10, of which 8 were waited for; matrix products, arithmetic and copies ran while one was open for 18% of the time, Pallas kernels for 0%

commit v1 on v0

v1 whole, which is shorter than its diff:
```python
import functools
import math

import jax
import jax.numpy as jnp
from jax import lax
from jax.experimental import pallas as pl
from jax.experimental.pallas import tpu as pltpu
from jax.sharding import PartitionSpec as P

LAYERS = 3
QPER = 5
HD = 128
PAGE = 4
REACH = 8
MESH = pl.DeviceIdType.MESH

masked_score = -16384.0
exponent_scale = math.log2(math.e) / math.sqrt(HD)


def ring_attention(
    seq_count, q_ref, k_ref, v_ref, len_ref, o_ref,
    qs, kbuf, vbuf, bias, eye, ones, top, acc, total, send_sem, recv_sem,
):
    rows = k_ref.shape[0]
    kv_local = kbuf.shape[0]
    mine = lax.axis_index("seq")
    right = lax.rem(mine + 1, seq_count)
    left = lax.rem(mine + seq_count - 1, seq_count)

    barrier = pltpu.get_barrier_semaphore()
    pl.semaphore_signal(barrier, inc=1, device_id={"seq": left}, device_id_type=MESH)
    pl.semaphore_wait(barrier, 1)

    def hop(part, c, slot):
        held = (kbuf, vbuf)[part]
        if isinstance(slot, int) and slot == 1:
            src = (k_ref, v_ref)[part].at[:, pl.ds(c * HD, HD)]
        else:
            src = held.at[c, pl.ds(pl.multiple_of((slot - 1) * rows, rows), rows)]
        return pltpu.make_async_remote_copy(
            src_ref=src,
            dst_ref=held.at[c, pl.ds(pl.multiple_of(slot * rows, rows), rows)],
            send_sem=send_sem.at[slot - 1, c, part],
            recv_sem=recv_sem.at[slot - 1, c, part],
            device_id={"seq": right},
            device_id_type=MESH,
        )

    pieces = [(part, c) for c in range(kv_local) for part in range(2)]
    for part, c in pieces:
        hop(part, c, 1).start()

    for c in range(kv_local):
        kbuf[c, pl.ds(0, rows)] = k_ref[:, c * HD:(c + 1) * HD]
        vbuf[c, pl.ds(0, rows)] = v_ref[:, c * HD:(c + 1) * HD]
        for layer in range(LAYERS):
            for i in range(QPER):
                h = c * QPER + i
                qs[c, layer, pl.ds(i * rows, rows)] = q_ref[layer, :, h * HD:(h + 1) * HD]
    reqs = len_ref.shape[1]
    lengths = len_ref[...].astype(jnp.float32)
    before = lax.broadcasted_iota(jnp.int32, (reqs, reqs), 1) < lax.broadcasted_iota(
        jnp.int32, (reqs, reqs), 0
    )
    starts = jnp.sum(
        jnp.where(before, jnp.broadcast_to(lengths, (reqs, reqs)), 0.0), axis=1, keepdims=True
    )
    query_pos = (mine * rows + lax.broadcasted_iota(jnp.int32, (reqs, rows), 1)).astype(jnp.float32)
    began = jnp.max(jnp.where(starts <= query_pos, starts, 0.0), axis=0, keepdims=True)
    token = (mine * rows + lax.broadcasted_iota(jnp.int32, (rows, rows), 1)).astype(jnp.float32)
    row_iota = lax.broadcasted_iota(jnp.int32, (rows, rows), 0)
    for d in range(REACH + 1):
        key_pos = ((mine - d) * rows + row_iota).astype(jnp.float32)
        allowed = (key_pos >= began) & (key_pos <= token)
        bias[pl.ds(d * rows, rows)] = jnp.where(allowed, 0.0, masked_score).astype(jnp.bfloat16)
    same = (row_iota == lax.broadcasted_iota(jnp.int32, (rows, rows), 1)).astype(jnp.bfloat16)
    for i in range(QPER):
        eye[pl.ds(i * rows, rows)] = same.astype(jnp.bfloat16)
    ones[...] = jnp.ones_like(ones)
    top[...] = jnp.full_like(top, -1e30)
    acc[...] = jnp.zeros_like(acc)
    total[...] = jnp.zeros_like(total)

    def piece(c, layer, first, count):
        span = pl.ds(first, count)
        wide_q = jnp.concatenate([qs[c, layer], eye[...]], axis=1)
        wide_k = jnp.concatenate([kbuf[c, span], bias[span]], axis=1)
        scores = lax.dot_general(
            wide_q, wide_k, (((1,), (1,)), ((), ())), preferred_element_type=jnp.float32
        )
        old = top[c, layer]
        fresh = jnp.maximum(old, jnp.max(scores, axis=1, keepdims=True))
        weights = jnp.exp2((scores - fresh[:, :1]) * exponent_scale)
        shrink = jnp.exp2((old - fresh) * exponent_scale)
        wide_v = jnp.concatenate([vbuf[c, span], ones[pl.ds(0, count)]], axis=1)
        product = jnp.dot(weights.astype(jnp.bfloat16), wide_v, preferred_element_type=jnp.float32)
        top[c, layer] = fresh
        acc[c, layer] = acc[c, layer] * shrink + product[:, :HD]
        total[c, layer] = total[c, layer] * shrink + product[:, HD:]

    def receive(slot, forward):
        for part, c in pieces:
            hop(part, c, slot).wait_recv()
            if forward:
                hop(part, c, slot + 1).start()

    receive(1, True)

    def step(j, carry):
        receive(j + 2, True)
        c = lax.rem(j, kv_local)
        first = pl.multiple_of((j // kv_local) * 2 * rows, 2 * rows)

        def one_layer(layer, carry):
            piece(c, layer, first, 2 * rows)
            return carry

        return lax.fori_loop(0, LAYERS, one_layer, carry)

    lax.fori_loop(0, REACH - 2, step, 0)
    receive(REACH, False)
    near = (REACH - 2) * rows

    def last(layer, carry):
        for c in range(kv_local):
            piece(c, layer, near, 3 * rows)
            done = acc[c, layer] / total[c, layer]
            for i in range(QPER):
                h = c * QPER + i
                o_ref[layer, :, h * HD:(h + 1) * HD] = done[i * rows:(i + 1) * rows].astype(o_ref.dtype)
        return carry

    lax.fori_loop(0, LAYERS, last, 0)
    for slot in range(1, REACH + 1):
        for part, c in pieces:
            hop(part, c, slot).wait_send()


def attend(queries, keys, values, lengths):
    rows = keys.shape[0]
    kv_local = keys.shape[1] // HD
    seq_count = lax.axis_size("seq")
    width = queries.shape[2]
    wide = QPER * rows
    out = pl.pallas_call(
        functools.partial(ring_attention, seq_count),
        name="ring_attention",
        out_shape=jax.ShapeDtypeStruct((LAYERS, rows, width), jnp.bfloat16),
        in_specs=[pl.BlockSpec(memory_space=pltpu.VMEM)] * 4,
        out_specs=pl.BlockSpec(memory_space=pltpu.VMEM),
        scratch_shapes=[
            pltpu.VMEM((kv_local, LAYERS, wide, HD), jnp.bfloat16),
            pltpu.VMEM((kv_local, (REACH + 1) * rows, HD), jnp.bfloat16),
            pltpu.VMEM((kv_local, (REACH + 1) * rows, HD), jnp.bfloat16),
            pltpu.VMEM(((REACH + 1) * rows, rows), jnp.bfloat16),
            pltpu.VMEM((wide, rows), jnp.bfloat16),
            pltpu.VMEM((3 * rows, HD), jnp.bfloat16),
            pltpu.VMEM((kv_local, LAYERS, wide, HD), jnp.float32),
            pltpu.VMEM((kv_local, LAYERS, wide, HD), jnp.float32),
            pltpu.VMEM((kv_local, LAYERS, wide, HD), jnp.float32),
            pltpu.SemaphoreType.DMA((REACH, kv_local, 2)),
            pltpu.SemaphoreType.DMA((REACH, kv_local, 2)),
        ],
        compiler_params=pltpu.CompilerParams(
            collective_id=0, has_side_effects=True, vmem_limit_bytes=56 * 1024 * 1024
        ),
    )(queries.transpose(1, 0, 2), keys, values, lengths.reshape(1, -1))
    return out.transpose(1, 0, 2)


def shards(queries, keys, values, lengths, page_owner, page_slot):
    tok_rows = keys.shape[0]
    kv_local = keys.shape[1] // HD
    seq_count = lax.axis_size("seq")
    pages_dev = tok_rows // PAGE
    slots = pages_dev * kv_local
    key_pages = keys.reshape(pages_dev, PAGE, kv_local, HD)
    val_pages = values.reshape(pages_dev, PAGE, kv_local, HD)
    flat_pages = (
        jnp.concatenate([key_pages, val_pages], axis=3)
        .transpose(0, 2, 1, 3)
        .reshape(slots, PAGE * 2 * HD)
    )
    owner = page_owner.reshape(slots)
    slot = page_slot.reshape(slots)
    number = jnp.arange(slots, dtype=jnp.int32)
    tag_lane = jnp.broadcast_to((slot + 1).astype(jnp.bfloat16)[:, None], (slots, HD))
    flat_pages = jnp.concatenate([flat_pages, tag_lane], axis=1)
    lanes = jnp.arange(seq_count, dtype=jnp.int32)
    picker = (lanes[:, None] == owner[None, :]).astype(jnp.bfloat16)
    outgoing = jnp.dot(picker, flat_pages, preferred_element_type=jnp.float32).astype(jnp.bfloat16)
    received = lax.all_to_all(
        outgoing.reshape(seq_count, 1, PAGE * 2 * HD + HD), "seq", split_axis=0, concat_axis=0, tiled=True
    ).reshape(seq_count, PAGE * 2 * HD + HD)
    got_tags = received[:, PAGE * 2 * HD].astype(jnp.int32)
    placer = (got_tags[None, :] == (number + 1)[:, None]).astype(jnp.bfloat16)
    cache_pages = jnp.dot(
        placer, received[:, :PAGE * 2 * HD], preferred_element_type=jnp.float32
    ).astype(jnp.bfloat16)
    cache_pages = cache_pages.reshape(slots, PAGE, 2 * HD)
    attended = attend(queries, keys, values, lengths)
    return (attended, cache_pages)


def solution(mesh):
    placed = (
        P(("group", "seq"), None, "head"),
        P(("group", "seq"), "head"),
        P(("group", "seq"), "head"),
        P("group"),
        P(("group", "seq"), "head"),
        P(("group", "seq"), "head"),
    )
    return jax.shard_map(
        shards,
        mesh=mesh,
        in_specs=placed,
        out_specs=(P(("group", "seq"), None, "head"), P(("group", "seq", "head"), None, None)),
        check_vma=False,
    )
```

time: 195 us -> 132 us (0.68)
  the two profiles are of different devices: /device:TPU:38 before, /device:TPU:40 now
where the time goes in v1:
time: 132 us; the launch traced here: 131 us
  Pallas kernels  68.3 us (52%)
  starting transfers between devices  53.2 us (40%)
  local copies, waits for them, and re-layouts  6.75 us (5%)
  other arithmetic  1.63 us (1%)
    pallas_call x1, Pallas kernels, attend(): pl.pallas_call(functools.partial(ring_attention, seq_count), name='ring_a...  68.3 us
    all_to_all x1, starting transfers between devices, shards(): lax.all_to_all(outgoing.reshape(seq_count, 1, PAGE * 2 * HD + HD), 'seq',...  53.2 us
    unnamed x12, local copies, waits for them, and re-layouts  4.17 us
  transfers between devices with their start and end apart: 1, of which 0 were waited for; matrix products, arithmetic and copies ran while one was open for 0% of the time, Pallas kernels for 52%

profile of v1, /device:TPU:40, one launch (start us, length us, event | category | flops | bytes accessed | tf_op | source)
XLA Modules:
  0.0 131.1 jit_solution(15221725348958497649)
XLA Ops:
  0.6 0.7 add_convert_fusion
  1.3 0.1 copy.22
  1.4 0.1 convert_element_type.29
  1.5 0.9 reshape.49
  2.4 0.0 copy-start.1
  2.4 0.8 copy-done.1
  3.3 0.1 pad_maximum_fusion
  3.4 0.0 copy-start.2
  3.4 0.6 copy-done.2
  4.0 0.1 copy.19
  4.1 0.1 eq.29
  4.2 0.1 broadcast_in_dim.2
  4.3 0.2 fusion
  4.5 0.5 broadcast.20
  5.1 0.8 reduce.2
  5.8 1.1 reshape.56
  6.9 53.2 %all-to-all-start = ((bf16[128,2,576]{2,1,0:T(2,128)(2,1)}), bf16[128,2,576]{2,1,0:T(2,128)(2,1)S(1)}, u32[]{:S(2)}, u32[]{:S(2)}) async-start(bf16[128,2,576]{2,1,0:T(2,128)(2,1)} %reshape.56), calls=%async_computation | async-start | bytes 655360 | tf_op jit(solution)/shard_map/all_to_all | solution.py:194
  60.1 68.3 %ring_attention.1 = bf16[3,128,1280]{2,1,0:T(8,128)(2,1)} custom-call(bf16[3,128,1280]{2,1,0:T(8,128)(2,1)} %bitcast.15, bf16[128,256]{1,0:T(8,128)(2,1)} %k_ref.1, bf16[128,256]{1,0:T(8,128)(2,1)} %v_ref.1, s32[1,64]{1,0:T(1,128)} %bitcast.18), custom_call_target="tpu_custom_call" | custom-call | tf_op jit(solution)/shard_map/ring_attention/pallas_call | solution.py:147
  128.4 0.0 all-to-all-done
  128.4 0.5 reshape.57
  129.0 0.0 copy-start
  129.0 0.1 convert_reduce_fusion
  129.1 0.2 convolution_convert_fusion.1
  129.4 0.7 reshape.53
  130.1 0.1 copy-done
  130.2 0.9 copy.30
  (6 shorter events, 0.1 us)
Async XLA Ops:
  2.4 0.8 copy-start.1
  3.4 0.7 copy-start.2
  6.9 121.5 %all-to-all-start = ((bf16[128,2,576]{2,1,0:T(2,128)(2,1)}), bf16[128,2,576]{2,1,0:T(2,128)(2,1)S(1)}, u32[]{:S(2)}, u32[]{:S(2)}) async-start(bf16[128,2,576]{2,1,0:T(2,128)(2,1)} %reshape.56), calls=%async_computation | async-start | bytes 655360 | tf_op jit(solution)/shard_map/all_to_all | solution.py:194
  129.0 1.2 copy-start

commit v2 on v1

--- a/solution.py
+++ b/solution.py
@@ -13,6 +13,7 @@
 HD = 128
 PAGE = 4
 REACH = 8
+GROUP = 3
 MESH = pl.DeviceIdType.MESH
 
 masked_score = -16384.0
@@ -21,10 +22,11 @@
 
 def ring_attention(
     seq_count, q_ref, k_ref, v_ref, len_ref, o_ref,
-    qs, kbuf, vbuf, bias, eye, ones, top, acc, total, send_sem, recv_sem,
+    qs, held, bias, eye, ones, top, acc, total, send_sem, recv_sem,
 ):
     rows = k_ref.shape[0]
-    kv_local = kbuf.shape[0]
+    kv_local = held.shape[1]
+    parts = 2 * kv_local
     mine = lax.axis_index("seq")
     right = lax.rem(mine + 1, seq_count)
     left = lax.rem(mine + seq_count - 1, seq_count)
@@ -33,28 +35,26 @@
     pl.semaphore_signal(barrier, inc=1, device_id={"seq": left}, device_id_type=MESH)
     pl.semaphore_wait(barrier, 1)
 
-    def hop(part, c, slot):
-        held = (kbuf, vbuf)[part]
-        if isinstance(slot, int) and slot == 1:
-            src = (k_ref, v_ref)[part].at[:, pl.ds(c * HD, HD)]
-        else:
-            src = held.at[c, pl.ds(pl.multiple_of((slot - 1) * rows, rows), rows)]
+    def hop(n, src=None):
+        slot = n // parts
+        c, part = (n % parts) // 2, n % 2
+        if src is None:
+            src = held.at[part, c, pl.ds(pl.multiple_of(slot * rows, rows), rows)]
         return pltpu.make_async_remote_copy(
             src_ref=src,
-            dst_ref=held.at[c, pl.ds(pl.multiple_of(slot * rows, rows), rows)],
-            send_sem=send_sem.at[slot - 1, c, part],
-            recv_sem=recv_sem.at[slot - 1, c, part],
+            dst_ref=held.at[part, c, pl.ds(pl.multiple_of((slot + 1) * rows, rows), rows)],
+            send_sem=send_sem.at[n],
+            recv_sem=recv_sem.at[n],
             device_id={"seq": right},
             device_id_type=MESH,
         )
 
-    pieces = [(part, c) for c in range(kv_local) for part in range(2)]
-    for part, c in pieces:
-        hop(part, c, 1).start()
+    for n in range(parts):
+        hop(n, (k_ref, v_ref)[n % 2].at[:, pl.ds((n // 2) * HD, HD)]).start()
 
     for c in range(kv_local):
-        kbuf[c, pl.ds(0, rows)] = k_ref[:, c * HD:(c + 1) * HD]
-        vbuf[c, pl.ds(0, rows)] = v_ref[:, c * HD:(c + 1) * HD]
+        held[0, c, pl.ds(0, rows)] = k_ref[:, c * HD:(c + 1) * HD]
+        held[1, c, pl.ds(0, rows)] = v_ref[:, c * HD:(c + 1) * HD]
         for layer in range(LAYERS):
             for i in range(QPER):
                 h = c * QPER + i
@@ -79,63 +79,80 @@
     for i in range(QPER):
         eye[pl.ds(i * rows, rows)] = same.astype(jnp.bfloat16)
     ones[...] = jnp.ones_like(ones)
-    top[...] = jnp.full_like(top, -1e30)
-    acc[...] = jnp.zeros_like(acc)
-    total[...] = jnp.zeros_like(total)
-
-    def piece(c, layer, first, count):
-        span = pl.ds(first, count)
+    span = GROUP * rows
+
+    def piece(i, first, last=False):
+        c, layer = i // LAYERS, i % LAYERS
+        keys = pl.ds(first * rows, span)
         wide_q = jnp.concatenate([qs[c, layer], eye[...]], axis=1)
-        wide_k = jnp.concatenate([kbuf[c, span], bias[span]], axis=1)
+        wide_k = jnp.concatenate([held[0, c, keys], bias[keys]], axis=1)
         scores = lax.dot_general(
             wide_q, wide_k, (((1,), (1,)), ((), ())), preferred_element_type=jnp.float32
         )
-        old = top[c, layer]
-        fresh = jnp.maximum(old, jnp.max(scores, axis=1, keepdims=True))
-        weights = jnp.exp2((scores - fresh[:, :1]) * exponent_scale)
-        shrink = jnp.exp2((old - fresh) * exponent_scale)
-        wide_v = jnp.concatenate([vbuf[c, span], ones[pl.ds(0, count)]], axis=1)
+        fresh = jnp.max(scores, axis=1, keepdims=True)
+        if first > 0:
+            old = top[c, layer]
+            fresh = jnp.maximum(old, fresh)
+            shrink = jnp.exp2((old - fresh) * exponent_scale)
+            fresh = fresh[:, :1]
+        weights = jnp.exp2((scores - fresh) * exponent_scale)
+        wide_v = jnp.concatenate([held[1, c, keys], ones[...]], axis=1)
         product = jnp.dot(weights.astype(jnp.bfloat16), wide_v, preferred_element_type=jnp.float32)
-        top[c, layer] = fresh
-        acc[c, layer] = acc[c, layer] * shrink + product[:, :HD]
-        total[c, layer] = total[c, layer] * shrink + product[:, HD:]
-
-    def receive(slot, forward):
-        for part, c in pieces:
-            hop(part, c, slot).wait_recv()
-            if forward:
-                hop(part, c, slot + 1).start()
-
-    receive(1, True)
-
-    def step(j, carry):
-        receive(j + 2, True)
-        c = lax.rem(j, kv_local)
-        first = pl.multiple_of((j // kv_local) * 2 * rows, 2 * rows)
-
-        def one_layer(layer, carry):
-            piece(c, layer, first, 2 * rows)
+        summed, counted = product[:, :HD], product[:, HD:]
+        if first > 0:
+            summed = acc[c, layer] * shrink + summed
+            counted = total[c, layer] * shrink + counted
+        if last:
+            done = (summed / counted).astype(o_ref.dtype)
+            for q in range(QPER):
+                h = c * QPER + q
+                place = h * HD if isinstance(h, int) else pl.multiple_of(h * HD, HD)
+                o_ref[layer, :, pl.ds(place, HD)] = done[q * rows:(q + 1) * rows]
+        else:
+            top[c, layer] = jnp.broadcast_to(fresh, (QPER * rows, HD))
+            acc[c, layer] = summed
+            total[c, layer] = counted
+
+    def handle(n, forward=True):
+        hop(n).wait_recv()
+        if forward:
+            hop(n + parts).start()
+
+    def loop(count, body):
+        def step(i, carry):
+            body(i)
             return carry
 
-        return lax.fori_loop(0, LAYERS, one_layer, carry)
-
-    lax.fori_loop(0, REACH - 2, step, 0)
-    receive(REACH, False)
-    near = (REACH - 2) * rows
-
-    def last(layer, carry):
-        for c in range(kv_local):
-            piece(c, layer, near, 3 * rows)
-            done = acc[c, layer] / total[c, layer]
-            for i in range(QPER):
-                h = c * QPER + i
-                o_ref[layer, :, h * HD:(h + 1) * HD] = done[i * rows:(i + 1) * rows].astype(o_ref.dtype)
-        return carry
-
-    lax.fori_loop(0, LAYERS, last, 0)
-    for slot in range(1, REACH + 1):
-        for part, c in pieces:
-            hop(part, c, slot).wait_send()
+        lax.fori_loop(0, count, step, 0)
+
+    loop(8, handle)
+
+    def first_group(i):
+        handle(8 + 2 * i)
+        piece(i, 0)
+        handle(9 + 2 * i)
+
+    loop(kv_local * LAYERS, first_group)
+
+    def second_group(i):
+        handle(20 + i)
+        piece(i, GROUP)
+
+    loop(kv_local * LAYERS, second_group)
+    handle(26)
+    handle(27)
+    handle(28, False)
+    handle(29, False)
+
+    def third_group(i):
+        @pl.when(i < 2)
+        def _():
+            handle(30 + i, False)
+
+        piece(i, 2 * GROUP, True)
+
+    loop(kv_local * LAYERS, third_group)
+    loop(REACH * parts, lambda n: hop(n).wait_send())
 
 
 def attend(queries, keys, values, lengths):
@@ -152,16 +169,15 @@
         out_specs=pl.BlockSpec(memory_space=pltpu.VMEM),
         scratch_shapes=[
             pltpu.VMEM((kv_local, LAYERS, wide, HD), jnp.bfloat16),
-            pltpu.VMEM((kv_local, (REACH + 1) * rows, HD), jnp.bfloat16),
-            pltpu.VMEM((kv_local, (REACH + 1) * rows, HD), jnp.bfloat16),
+            pltpu.VMEM((2, kv_local, (REACH + 1) * rows, HD), jnp.bfloat16),
             pltpu.VMEM(((REACH + 1) * rows, rows), jnp.bfloat16),
             pltpu.VMEM((wide, rows), jnp.bfloat16),
-            pltpu.VMEM((3 * rows, HD), jnp.bfloat16),
+            pltpu.VMEM((GROUP * rows, HD), jnp.bfloat16),
             pltpu.VMEM((kv_local, LAYERS, wide, HD), jnp.float32),
             pltpu.VMEM((kv_local, LAYERS, wide, HD), jnp.float32),
             pltpu.VMEM((kv_local, LAYERS, wide, HD), jnp.float32),
-            pltpu.SemaphoreType.DMA((REACH, kv_local, 2)),
-            pltpu.SemaphoreType.DMA((REACH, kv_local, 2)),
+            pltpu.SemaphoreType.DMA((REACH * kv_local * 2,)),
+            pltpu.SemaphoreType.DMA((REACH * kv_local * 2,)),
         ],
         compiler_params=pltpu.CompilerParams(
             collective_id=0, has_side_effects=True, vmem_limit_bytes=56 * 1024 * 1024

time: 132 us -> 129 us (0.977)
  Pallas kernels: 68.3 us -> 65.7 us
    pallas_call x1, Pallas kernels: 68.3 us -> 65.7 us  [attend(): pl.pallas_call(functools.partial(ring_attention, seq_count), name='ring_a...]
  transfers between devices with their start and end apart: 1 -> 1, of which waited for: 0 -> 0; matrix products, arithmetic and copies ran while one was open for 0% -> 0% of each run, Pallas kernels for 52% -> 51%
where the time goes in v2:
time: 129 us
  Pallas kernels  65.7 us (51%)
  starting transfers between devices  53.2 us (41%)
  local copies, waits for them, and re-layouts  6.75 us (5%)
  other arithmetic  1.63 us (1%)
    pallas_call x1, Pallas kernels, attend(): pl.pallas_call(functools.partial(ring_attention, seq_count), name='ring_a...  65.7 us
    all_to_all x1, starting transfers between devices, shards(): lax.all_to_all(outgoing.reshape(seq_count, 1, PAGE * 2 * HD + HD), 'seq',...  53.2 us
    unnamed x12, local copies, waits for them, and re-layouts  4.17 us
  transfers between devices with their start and end apart: 1, of which 0 were waited for; matrix products, arithmetic and copies ran while one was open for 0% of the time, Pallas kernels for 51%

profile of v2, /device:TPU:40, one launch (start us, length us, event | category | flops | bytes accessed | tf_op | source)
XLA Modules:
  0.0 128.5 jit_solution(9884474523298204469)
XLA Ops:
  0.6 0.7 add_convert_fusion
  1.3 0.1 copy.22
  1.4 0.1 convert_element_type.29
  1.5 0.9 reshape.49
  2.4 0.0 copy-start.1
  2.4 0.8 copy-done.1
  3.3 0.1 pad_maximum_fusion
  3.4 0.0 copy-start.2
  3.4 0.6 copy-done.2
  4.0 0.1 copy.19
  4.1 0.1 eq.29
  4.2 0.1 broadcast_in_dim.2
  4.3 0.2 fusion
  4.5 0.5 broadcast.20
  5.1 0.8 reduce.2
  5.8 1.1 reshape.56
  6.9 53.2 %all-to-all-start = ((bf16[128,2,576]{2,1,0:T(2,128)(2,1)}), bf16[128,2,576]{2,1,0:T(2,128)(2,1)S(1)}, u32[]{:S(2)}, u32[]{:S(2)}) async-start(bf16[128,2,576]{2,1,0:T(2,128)(2,1)} %reshape.56), calls=%async_computation | async-start | bytes 655360 | tf_op jit(solution)/shard_map/all_to_all | solution.py:210
  60.1 65.7 %ring_attention.1 = bf16[3,128,1280]{2,1,0:T(8,128)(2,1)} custom-call(bf16[3,128,1280]{2,1,0:T(8,128)(2,1)} %bitcast.15, bf16[128,256]{1,0:T(8,128)(2,1)} %k_ref.1, bf16[128,256]{1,0:T(8,128)(2,1)} %v_ref.1, s32[1,64]{1,0:T(1,128)} %bitcast.18), custom_call_target="tpu_custom_call" | custom-call | tf_op jit(solution)/shard_map/ring_attention/pallas_call | solution.py:164
  125.8 0.0 all-to-all-done
  125.8 0.5 reshape.57
  126.4 0.0 copy-start
  126.4 0.1 convert_reduce_fusion
  126.5 0.2 convolution_convert_fusion.1
  126.8 0.7 reshape.53
  127.5 0.1 copy-done
  127.6 0.9 copy.30
  (6 shorter events, 0.1 us)
Async XLA Ops:
  2.4 0.8 copy-start.1
  3.4 0.7 copy-start.2
  6.9 118.9 %all-to-all-start = ((bf16[128,2,576]{2,1,0:T(2,128)(2,1)}), bf16[128,2,576]{2,1,0:T(2,128)(2,1)S(1)}, u32[]{:S(2)}, u32[]{:S(2)}) async-start(bf16[128,2,576]{2,1,0:T(2,128)(2,1)} %reshape.56), calls=%async_computation | async-start | bytes 655360 | tf_op jit(solution)/shard_map/all_to_all | solution.py:210
  126.4 1.2 copy-start

commit v3 on v2

--- a/solution.py
+++ b/solution.py
@@ -14,6 +14,8 @@
 PAGE = 4
 REACH = 8
 GROUP = 3
+COLUMNS = 4
+FIRST_HOPS = 6
 MESH = pl.DeviceIdType.MESH
 
 masked_score = -16384.0
@@ -21,8 +23,10 @@
 
 
 def ring_attention(
-    seq_count, q_ref, k_ref, v_ref, len_ref, o_ref,
+    seq_count, q_ref, k_ref, v_ref, len_ref, owner_ref, slot_ref, o_ref, page_ref,
     qs, held, bias, eye, ones, top, acc, total, send_sem, recv_sem,
+    picked, across, along, landed, tag_across, tag_along, tag_landed,
+    across_send, across_recv, along_send, along_recv, from_right, from_left,
 ):
     rows = k_ref.shape[0]
     kv_local = held.shape[1]
@@ -31,9 +35,27 @@
     right = lax.rem(mine + 1, seq_count)
     left = lax.rem(mine + seq_count - 1, seq_count)
 
+    places = seq_count // COLUMNS
+    column, place = mine // places, lax.rem(mine, places)
+
+    def at_place(offset):
+        return column * places + lax.rem(place + places + offset, places)
+
+    def at_column(offset):
+        return lax.rem(column + COLUMNS + offset, COLUMNS) * places + place
+
+    def signal(sem, device):
+        pl.semaphore_signal(sem, inc=1, device_id={"seq": device}, device_id_type=MESH)
+
     barrier = pltpu.get_barrier_semaphore()
-    pl.semaphore_signal(barrier, inc=1, device_id={"seq": left}, device_id_type=MESH)
-    pl.semaphore_wait(barrier, 1)
+    signal(barrier, left)
+    signal(barrier, at_place(1))
+    signal(barrier, at_place(-1))
+    for offset in range(1, COLUMNS):
+        signal(barrier, at_column(offset))
+    pl.semaphore_wait(barrier, COLUMNS + 2)
+    signal(from_right, at_place(-1))
+    signal(from_left, at_place(1))
 
     def hop(n, src=None):
         slot = n // parts
@@ -51,6 +73,95 @@
 
     for n in range(parts):
         hop(n, (k_ref, v_ref)[n % 2].at[:, pl.ds((n // 2) * HD, HD)]).start()
+
+    lines = places * PAGE
+    unit = COLUMNS * PAGE
+
+    def iota(shape, axis):
+        return lax.broadcasted_iota(jnp.int32, shape, axis)
+
+    pages_dev = rows // PAGE
+    widen = (iota((pages_dev, rows), 0) == iota((pages_dev, rows), 1) // PAGE).astype(jnp.bfloat16)
+
+    def per_token(ref):
+        wide = jnp.dot(
+            ref[...].astype(jnp.float32).astype(jnp.bfloat16), widen, preferred_element_type=jnp.float32
+        )
+        return jnp.concatenate([wide[c:c + 1] for c in range(kv_local)], axis=1)
+
+    owner_row = per_token(owner_ref)
+    slot_row = per_token(slot_ref) + 1.0
+    line_row = (iota((1, kv_local * rows), 1) % PAGE).astype(jnp.float32)
+    goes = iota((seq_count * PAGE, kv_local * rows), 0).astype(jnp.float32) == owner_row * PAGE + line_row
+    source = jnp.concatenate(
+        [
+            jnp.concatenate(
+                [k_ref[:, c * HD:(c + 1) * HD], v_ref[:, c * HD:(c + 1) * HD]], axis=1
+            )
+            for c in range(kv_local)
+        ],
+        axis=0,
+    )
+
+    def one_hot(mask):
+        return jnp.where(mask, 1.0, 0.0).astype(jnp.bfloat16)
+
+    picked[...] = jnp.dot(one_hot(goes), source, preferred_element_type=jnp.float32).astype(jnp.bfloat16)
+    owned = (iota((seq_count, kv_local * rows), 0).astype(jnp.float32) == owner_row) & (
+        jnp.broadcast_to(line_row, (seq_count, kv_local * rows)) == 0.0
+    )
+    tags = lax.dot_general(
+        jnp.broadcast_to(slot_row, (8, kv_local * rows)).astype(jnp.bfloat16),
+        one_hot(owned),
+        (((1,), (1,)), ((), ())),
+        preferred_element_type=jnp.float32,
+    )
+    tag_across[column] = tags[:1]
+    own_lines = pl.ds(pl.multiple_of(column * lines, lines), lines)
+    across[own_lines] = picked[own_lines]
+
+    def to_column(offset):
+        device = at_column(offset)
+        first = pl.multiple_of((device // places) * lines, lines)
+        return [
+            pltpu.make_async_remote_copy(
+                src_ref=src,
+                dst_ref=dst,
+                send_sem=across_send.at[part, offset],
+                recv_sem=across_recv.at[part, offset],
+                device_id={"seq": device},
+                device_id_type=MESH,
+            )
+            for part, (src, dst) in enumerate(
+                (
+                    (picked.at[pl.ds(first, lines)], across.at[own_lines]),
+                    (tag_across.at[column], tag_across.at[column]),
+                )
+            )
+        ]
+
+    def to_place(offset, landing):
+        device = at_place(offset)
+        there = lax.rem(device, places)
+        return [
+            pltpu.make_async_remote_copy(
+                src_ref=src,
+                dst_ref=dst,
+                send_sem=along_send.at[part, landing],
+                recv_sem=along_recv.at[part, landing],
+                device_id={"seq": device},
+                device_id_type=MESH,
+            )
+            for part, (src, dst) in enumerate(
+                (
+                    (
+                        along.at[pl.ds(pl.multiple_of(there * unit, unit), unit)],
+                        landed.at[pl.ds(pl.multiple_of(landing * unit, unit), unit)],
+                    ),
+                    (tag_along.at[there], tag_landed.at[landing]),
+                )
+            )
+        ]
 
     for c in range(kv_local):
         held[0, c, pl.ds(0, rows)] = k_ref[:, c * HD:(c + 1) * HD]
@@ -125,48 +236,147 @@
 
         lax.fori_loop(0, count, step, 0)
 
-    loop(8, handle)
+    for offset in range(1, COLUMNS):
+        for copy in to_column(offset):
+            copy.start()
+
+    half = places // 2
+
+    def next_token(more):
+        pl.semaphore_wait(from_right, 1)
+        pl.semaphore_wait(from_left, 1)
+
+        @pl.when(more)
+        def _():
+            signal(from_right, at_place(-1))
+            signal(from_left, at_place(1))
+
+    def send_both(k):
+        for copy in to_place(k, k):
+            copy.start()
+
+        @pl.when(k < half)
+        def _():
+            for copy in to_place(-k, half + k):
+                copy.start()
+
+    def early(i):
+        next_token(i >= 0)
+        handle(i)
+
+    loop(FIRST_HOPS - 1, early)
+    for offset in range(1, COLUMNS):
+        for copy in to_column(offset):
+            copy.wait_recv()
+    row = iota((seq_count * PAGE, seq_count * PAGE), 0)
+    regroup = (row % unit) // PAGE * lines + row // unit * PAGE + row % PAGE
+    along[...] = jnp.dot(
+        one_hot(regroup == iota((seq_count * PAGE, seq_count * PAGE), 1)),
+        across[...],
+        preferred_element_type=jnp.float32,
+    ).astype(jnp.bfloat16)
+    tag_rows = jnp.zeros((HD, seq_count), jnp.float32)
+    for x in range(COLUMNS):
+        mask = (iota((HD, seq_count), 0) % unit) // PAGE == x
+        tag_rows = jnp.where(mask, jnp.broadcast_to(tag_across[x], (HD, seq_count)), tag_rows)
+    choose = iota((places, seq_count), 1) == column * places + iota((places, seq_count), 0)
+    tag_table = lax.dot_general(
+        one_hot(choose),
+        tag_rows.astype(jnp.bfloat16),
+        (((1,), (1,)), ((), ())),
+        preferred_element_type=jnp.float32,
+    )
+    for z in range(places):
+        tag_along[z] = tag_table[z:z + 1]
+    landed[pl.ds(0, unit)] = along[pl.ds(pl.multiple_of(place * unit, unit), unit)]
+    tag_landed[0] = tag_along[place]
+    loop(FIRST_HOPS, lambda i: send_both(i + 1))
+
+    def late(i):
+        k = i + FIRST_HOPS + 1
+        next_token(k < half)
+        handle(k - 2)
+        send_both(k)
+
+    loop(half - FIRST_HOPS, late)
+    done_chunks = half - 1
+    pieces = kv_local * LAYERS
 
     def first_group(i):
-        handle(8 + 2 * i)
+        handle(done_chunks + i)
         piece(i, 0)
-        handle(9 + 2 * i)
-
-    loop(kv_local * LAYERS, first_group)
+
+    loop(pieces, first_group)
 
     def second_group(i):
-        handle(20 + i)
+        handle(done_chunks + pieces + i)
         piece(i, GROUP)
 
-    loop(kv_local * LAYERS, second_group)
-    handle(26)
-    handle(27)
-    handle(28, False)
-    handle(29, False)
+    loop(pieces, second_group)
+    last_chunks = (REACH - 1) * parts
+    for n in range(done_chunks + 2 * pieces, last_chunks + 2):
+        handle(n, n < last_chunks)
+
+    def wait_pages(i):
+        for copy in to_place(1, i + 1):
+            copy.wait_recv()
+
+    loop(places - 1, wait_pages)
+    came = jnp.concatenate([tag_landed[z] for z in range(places)], axis=0)
+    spread = jnp.dot(
+        one_hot(iota((seq_count * PAGE, places), 0) // unit == iota((seq_count * PAGE, places), 1)),
+        came.astype(jnp.bfloat16),
+        preferred_element_type=jnp.float32,
+    )
+    here = iota((seq_count * PAGE, HD), 0) % unit == iota((seq_count * PAGE, HD), 1)
+    tag_column = jnp.sum(jnp.where(here, spread, 0.0), axis=1, keepdims=True)
+    line_column = (iota((seq_count * PAGE, 1), 0) % PAGE).astype(jnp.float32)
+    lands = (tag_column - 1.0) * PAGE + line_column
+    slot_lines = page_ref.shape[0]
+    put = iota((seq_count * PAGE, slot_lines), 1).astype(jnp.float32) == lands
+    page_ref[...] = lax.dot_general(
+        one_hot(put), landed[...], (((0,), (0,)), ((), ())), preferred_element_type=jnp.float32
+    ).astype(page_ref.dtype)
 
     def third_group(i):
         @pl.when(i < 2)
         def _():
-            handle(30 + i, False)
+            handle(last_chunks + 2 + i, False)
 
         piece(i, 2 * GROUP, True)
 
-    loop(kv_local * LAYERS, third_group)
+    loop(pieces, third_group)
     loop(REACH * parts, lambda n: hop(n).wait_send())
-
-
-def attend(queries, keys, values, lengths):
+    for offset in range(1, COLUMNS):
+        for copy in to_column(offset):
+            copy.wait_send()
+
+    def wait_sent(i):
+        for copy in to_place(1, i + 1):
+            copy.wait_send()
+
+    loop(places - 1, wait_sent)
+
+
+def shards(queries, keys, values, lengths, page_owner, page_slot):
     rows = keys.shape[0]
     kv_local = keys.shape[1] // HD
     seq_count = lax.axis_size("seq")
     width = queries.shape[2]
     wide = QPER * rows
-    out = pl.pallas_call(
+    pages_dev = rows // PAGE
+    slots = pages_dev * kv_local
+    places = seq_count // COLUMNS
+    lines = seq_count * PAGE
+    attended, pages = pl.pallas_call(
         functools.partial(ring_attention, seq_count),
         name="ring_attention",
-        out_shape=jax.ShapeDtypeStruct((LAYERS, rows, width), jnp.bfloat16),
-        in_specs=[pl.BlockSpec(memory_space=pltpu.VMEM)] * 4,
-        out_specs=pl.BlockSpec(memory_space=pltpu.VMEM),
+        out_shape=(
+            jax.ShapeDtypeStruct((LAYERS, rows, width), jnp.bfloat16),
+            jax.ShapeDtypeStruct((slots * PAGE, 2 * HD), jnp.bfloat16),
+        ),
+        in_specs=[pl.BlockSpec(memory_space=pltpu.VMEM)] * 6,
+        out_specs=(pl.BlockSpec(memory_space=pltpu.VMEM), pl.BlockSpec(memory_space=pltpu.VMEM)),
         scratch_shapes=[
             pltpu.VMEM((kv_local, LAYERS, wide, HD), jnp.bfloat16),
             pltpu.VMEM((2, kv_local, (REACH + 1) * rows, HD), jnp.bfloat16),
@@ -178,46 +388,28 @@
             pltpu.VMEM((kv_local, LAYERS, wide, HD), jnp.float32),
             pltpu.SemaphoreType.DMA((REACH * kv_local * 2,)),
             pltpu.SemaphoreType.DMA((REACH * kv_local * 2,)),
+            pltpu.VMEM((lines, 2 * HD), jnp.bfloat16),
+            pltpu.VMEM((lines, 2 * HD), jnp.bfloat16),
+            pltpu.VMEM((lines, 2 * HD), jnp.bfloat16),
+            pltpu.VMEM((lines, 2 * HD), jnp.bfloat16),
+            pltpu.VMEM((COLUMNS, 1, seq_count), jnp.float32),
+            pltpu.VMEM((places, 1, HD), jnp.float32),
+            pltpu.VMEM((places, 1, HD), jnp.float32),
+            pltpu.SemaphoreType.DMA((2, COLUMNS)),
+            pltpu.SemaphoreType.DMA((2, COLUMNS)),
+            pltpu.SemaphoreType.DMA((2, places)),
+            pltpu.SemaphoreType.DMA((2, places)),
+            pltpu.SemaphoreType.REGULAR,
+            pltpu.SemaphoreType.REGULAR,
         ],
         compiler_params=pltpu.CompilerParams(
             collective_id=0, has_side_effects=True, vmem_limit_bytes=56 * 1024 * 1024
         ),
-    )(queries.transpose(1, 0, 2), keys, values, lengths.reshape(1, -1))
-    return out.transpose(1, 0, 2)
-
-
-def shards(queries, keys, values, lengths, page_owner, page_slot):
-    tok_rows = keys.shape[0]
-    kv_local = keys.shape[1] // HD
-    seq_count = lax.axis_size("seq")
-    pages_dev = tok_rows // PAGE
-    slots = pages_dev * kv_local
-    key_pages = keys.reshape(pages_dev, PAGE, kv_local, HD)
-    val_pages = values.reshape(pages_dev, PAGE, kv_local, HD)
-    flat_pages = (
-        jnp.concatenate([key_pages, val_pages], axis=3)
-        .transpose(0, 2, 1, 3)
-        .reshape(slots, PAGE * 2 * HD)
-    )
-    owner = page_owner.reshape(slots)
-    slot = page_slot.reshape(slots)
-    number = jnp.arange(slots, dtype=jnp.int32)
-    tag_lane = jnp.broadcast_to((slot + 1).astype(jnp.bfloat16)[:, None], (slots, HD))
-    flat_pages = jnp.concatenate([flat_pages, tag_lane], axis=1)
-    lanes = jnp.arange(seq_count, dtype=jnp.int32)
-    picker = (lanes[:, None] == owner[None, :]).astype(jnp.bfloat16)
-    outgoing = jnp.dot(picker, flat_pages, preferred_element_type=jnp.float32).astype(jnp.bfloat16)
-    received = lax.all_to_all(
-        outgoing.reshape(seq_count, 1, PAGE * 2 * HD + HD), "seq", split_axis=0, concat_axis=0, tiled=True
-    ).reshape(seq_count, PAGE * 2 * HD + HD)
-    got_tags = received[:, PAGE * 2 * HD].astype(jnp.int32)
-    placer = (got_tags[None, :] == (number + 1)[:, None]).astype(jnp.bfloat16)
-    cache_pages = jnp.dot(
-        placer, received[:, :PAGE * 2 * HD], preferred_element_type=jnp.float32
-    ).astype(jnp.bfloat16)
-    cache_pages = cache_pages.reshape(slots, PAGE, 2 * HD)
-    attended = attend(queries, keys, values, lengths)
-    return (attended, cache_pages)
+    )(
+        queries.transpose(1, 0, 2), keys, values, lengths.reshape(1, -1),
+        page_owner.transpose(1, 0), page_slot.transpose(1, 0),
+    )
+    return (attended.transpose(1, 0, 2), pages.reshape(slots, PAGE, 2 * HD))
 
 
 def solution(mesh):

time: 129 us -> 113 us (0.88)
  starting transfers between devices: 53.2 us -> 0 us
  Pallas kernels: 65.7 us -> 109 us
  local copies, waits for them, and re-layouts: 6.75 us -> 3.8 us
  other arithmetic: 1.63 us -> 0 us
    all_to_all x1 -> x0, starting transfers between devices: 53.2 us -> none  [shards(): lax.all_to_all(outgoing.reshape(seq_count, 1, PAGE * 2 * HD + HD), 'seq',...]
    pallas_call x1, Pallas kernels: 65.7 us -> 109 us  [shards(): pl.pallas_call(functools.partial(ring_attention, seq_count), name='ring_a...]
    unnamed x12 -> x1, local copies, waits for them, and re-layouts: 4.17 us -> 2.21 us
  transfers between devices with their start and end apart: 1 -> 0, of which waited for: 0 -> 0; matrix products, arithmetic and copies ran while one was open for 0% -> 0% of each run, Pallas kernels for 51% -> 0%
where the time goes in v3:
time: 113 us
  Pallas kernels  109 us (96%)
  local copies, waits for them, and re-layouts  3.8 us (3%)
    pallas_call x1, Pallas kernels, shards(): pl.pallas_call(functools.partial(ring_attention, seq_count), name='ring_a...  109 us

profile of v3, /device:TPU:40, one launch (start us, length us, event | category | flops | bytes accessed | tf_op | source)
XLA Modules:
  0.0 113.0 jit_solution(9154196739382780697)
XLA Ops:
  0.6 108.6 %ring_attention.1 = (bf16[3,128,1280]{2,1,0:T(8,128)(2,1)}, bf16[256,256]{1,0:T(8,128)(2,1)}) custom-call(bf16[3,128,1280]{2,1,0:T(8,128)(2,1)} %bitcast.5, bf16[128,256]{1,0:T(8,128)(2,1)} %k_ref.1, bf16[128,256]{1,0:T(8,128)(2,1)} %v_ref.1, s32[1,64]{1,0:T(1,128)} %bitcast.9, s32[2,32]{1,0:T(2,128)} %bitcast.7, s32[2,32]{1,0:T(2,128)} %bitcast.8), custom_call_target="tpu_custom_call" | custom-call | tf_op jit(solution)/shard_map/ring_attention/pallas_call | solution.py:371
  109.2 1.6 %reshape.11 = bf16[64,4,256]{2,1,0:T(4,128)(2,1)} reshape(bf16[256,256]{1,0:T(8,128)(2,1)} %get-tuple-element.5) | data formatting | bytes 262144 | tf_op jit(solution)/shard_map/reshape | solution.py:412
  110.8 2.2 %copy.9 = bf16[128,3,1280]{2,0,1:T(8,128)(2,1)} copy(bf16[128,3,1280]{2,0,1:T(8,128)(2,1)} %bitcast.6) | data formatting | bytes 1966080

commit v4 on v3

--- a/solution.py
+++ b/solution.py
@@ -15,7 +15,8 @@
 REACH = 8
 GROUP = 3
 COLUMNS = 4
-FIRST_HOPS = 6
+STOP = 8
+FORWARD = 12
 MESH = pl.DeviceIdType.MESH
 
 masked_score = -16384.0
@@ -26,7 +27,8 @@
     seq_count, q_ref, k_ref, v_ref, len_ref, owner_ref, slot_ref, o_ref, page_ref,
     qs, held, bias, eye, ones, top, acc, total, send_sem, recv_sem,
     picked, across, along, landed, tag_across, tag_along, tag_landed,
-    across_send, across_recv, along_send, along_recv, from_right, from_left,
+    stopped, tag_stopped,
+    across_send, across_recv, along_send, along_recv, stop_send, stop_recv, from_right, from_left,
 ):
     rows = k_ref.shape[0]
     kv_local = held.shape[1]
@@ -241,6 +243,7 @@
             copy.start()
 
     half = places // 2
+    detour = half - FORWARD
 
     def next_token(more):
         pl.semaphore_wait(from_right, 1)
@@ -252,19 +255,61 @@
             signal(from_left, at_place(1))
 
     def send_both(k):
-        for copy in to_place(k, k):
+        for copy in to_place(-k, half + k):
             copy.start()
 
-        @pl.when(k < half)
+        @pl.when(k <= FORWARD)
         def _():
-            for copy in to_place(-k, half + k):
+            for copy in to_place(k, k):
                 copy.start()
+
+    def to_stop(j):
+        there = lax.rem(place + FORWARD + 1 + j, places)
+        here = pl.ds(pl.multiple_of(there * unit, unit), unit)
+        return [
+            pltpu.make_async_remote_copy(
+                src_ref=src,
+                dst_ref=dst,
+                send_sem=stop_send.at[part, j],
+                recv_sem=stop_recv.at[part, j],
+                device_id={"seq": at_place(-STOP)},
+                device_id_type=MESH,
+            )
+            for part, (src, dst) in enumerate(
+                (
+                    (along.at[here], stopped.at[pl.ds(pl.multiple_of(j * unit, unit), unit)]),
+                    (tag_along.at[there], tag_stopped.at[j]),
+                )
+            )
+        ]
+
+    def from_stop(j):
+        landing = FORWARD + 1 + j
+        return [
+            pltpu.make_async_remote_copy(
+                src_ref=src,
+                dst_ref=dst,
+                send_sem=along_send.at[part, landing],
+                recv_sem=along_recv.at[part, landing],
+                device_id={"seq": at_place(STOP + landing - places)},
+                device_id_type=MESH,
+            )
+            for part, (src, dst) in enumerate(
+                (
+                    (
+                        stopped.at[pl.ds(pl.multiple_of(j * unit, unit), unit)],
+                        landed.at[pl.ds(pl.multiple_of(landing * unit, unit), unit)],
+                    ),
+                    (tag_stopped.at[j], tag_landed.at[landing]),
+                )
+            )
+        ]
 
     def early(i):
         next_token(i >= 0)
         handle(i)
 
-    loop(FIRST_HOPS - 1, early)
+    loop(STOP - 1, early)
     for offset in range(1, COLUMNS):
         for copy in to_column(offset):
             copy.wait_recv()
@@ -290,16 +335,24 @@
         tag_along[z] = tag_table[z:z + 1]
     landed[pl.ds(0, unit)] = along[pl.ds(pl.multiple_of(place * unit, unit), unit)]
     tag_landed[0] = tag_along[place]
-    loop(FIRST_HOPS, lambda i: send_both(i + 1))
+    for j in range(detour):
+        for copy in to_stop(j):
+            copy.start()
+    loop(STOP, lambda i: send_both(i + 1))
 
     def late(i):
-        k = i + FIRST_HOPS + 1
-        next_token(k < half)
+        k = i + STOP + 1
+        next_token(k < half - 1)
         handle(k - 2)
         send_both(k)
 
-    loop(half - FIRST_HOPS, late)
-    done_chunks = half - 1
+    loop(half - 1 - STOP, late)
+    for j in range(detour):
+        for copy in to_stop(j):
+            copy.wait_recv()
+        for copy in from_stop(j):
+            copy.start()
+    done_chunks = half - 2
     pieces = kv_local * LAYERS
 
     def first_group(i):
@@ -356,6 +409,9 @@
             copy.wait_send()
 
     loop(places - 1, wait_sent)
+    for j in range(detour):
+        for copy in to_stop(j):
+            copy.wait_send()
 
 
 def shards(queries, keys, values, lengths, page_owner, page_slot):
@@ -368,6 +424,7 @@
     slots = pages_dev * kv_local
     places = seq_count // COLUMNS
     lines = seq_count * PAGE
+    detour = places // 2 - FORWARD
     attended, pages = pl.pallas_call(
         functools.partial(ring_attention, seq_count),
         name="ring_attention",
@@ -395,15 +452,19 @@
             pltpu.VMEM((COLUMNS, 1, seq_count), jnp.float32),
             pltpu.VMEM((places, 1, HD), jnp.float32),
             pltpu.VMEM((places, 1, HD), jnp.float32),
+            pltpu.VMEM((detour * COLUMNS * PAGE, 2 * HD), jnp.bfloat16),
+            pltpu.VMEM((detour, 1, HD), jnp.float32),
             pltpu.SemaphoreType.DMA((2, COLUMNS)),
             pltpu.SemaphoreType.DMA((2, COLUMNS)),
             pltpu.SemaphoreType.DMA((2, places)),
             pltpu.SemaphoreType.DMA((2, places)),
+            pltpu.SemaphoreType.DMA((2, detour)),
+            pltpu.SemaphoreType.DMA((2, detour)),
             pltpu.SemaphoreType.REGULAR,
             pltpu.SemaphoreType.REGULAR,
         ],
         compiler_params=pltpu.CompilerParams(
-            collective_id=0, has_side_effects=True, vmem_limit_bytes=56 * 1024 * 1024
+            collective_id=0, has_side_effects=True, vmem_limit_bytes=28 * 1024 * 1024
         ),
     )(
         queries.transpose(1, 0, 2), keys, values, lengths.reshape(1, -1),

time: 113 us -> 105 us (0.929)
  Pallas kernels: 109 us -> 99.2 us
  local copies, waits for them, and re-layouts: 3.8 us -> 5.19 us
    pallas_call x1, Pallas kernels: 109 us -> 99.2 us  [shards(): pl.pallas_call(functools.partial(ring_attention, seq_count), name='ring_a...]
    unnamed x1 -> x13, local copies, waits for them, and re-layouts: 2.21 us -> 4.5 us
where the time goes in v4:
time: 105 us
  Pallas kernels  99.2 us (94%)
  local copies, waits for them, and re-layouts  5.19 us (5%)
    pallas_call x1, Pallas kernels, shards(): pl.pallas_call(functools.partial(ring_attention, seq_count), name='ring_a...  99.2 us
    unnamed x13, local copies, waits for them, and re-layouts  4.5 us

profile of v4, /device:TPU:40, one launch (start us, length us, event | category | flops | bytes accessed | tf_op | source)
XLA Modules:
  0.0 105.1 jit_solution(15085441576974982875)
XLA Ops:
  0.6 0.0 copy-start.4
  0.6 0.0 copy-start.3
  0.7 0.0 copy-start.5
  0.7 0.7 copy-done.4
  1.3 0.0 copy-done.3
  1.3 0.0 copy-done.5
  1.3 0.0 copy-start
  1.3 1.2 %copy-done = bf16[128,3,1280]{2,0,1:T(8,128)(2,1)S(1)} copy-done((bf16[128,3,1280]{2,0,1:T(8,128)(2,1)S(1)}, bf16[128,3,1280]{2,0,1:T(8,128)(2,1)}, u32[]{:S(2)}) %copy-start) | copy-done | bytes 983064
  2.5 0.0 copy-start.1
  2.5 0.8 copy-done.1
  3.4 0.0 copy-start.2
  3.4 0.8 copy-done.2
  4.2 99.2 %ring_attention.1 = (bf16[3,128,1280]{2,1,0:T(8,128)(2,1)S(1)}, bf16[256,256]{1,0:T(8,128)(2,1)S(1)}) custom-call(bf16[3,128,1280]{2,1,0:T(8,128)(2,1)S(1)} %bitcast.5, bf16[128,256]{1,0:T(8,128)(2,1)S(1)} %copy-done.1, bf16[128,256]{1,0:T(8,128)(2,1)S(1)} %copy-done.2, s32[1,64]{1,0:T(1,128)S(1)} %bitcast.9, s32[2,32]{1,0:T(2,128)S(1)} %bitcast.7, ...), custom_call_target="tpu_custom_call" | custom-call | tf_op jit(solution)/shard_map/ring_attention/pallas_call | solution.py:428
  103.5 0.7 reshape.11
  104.2 0.9 copy.9
Async XLA Ops:
  0.6 0.7 copy-start.4
  0.6 0.7 copy-start.3
  0.7 0.7 copy-start.5
  1.3 1.2 %copy-start = (bf16[128,3,1280]{2,0,1:T(8,128)(2,1)S(1)}, bf16[128,3,1280]{2,0,1:T(8,128)(2,1)}, u32[]{:S(2)}) copy-start(bf16[128,3,1280]{2,0,1:T(8,128)(2,1)} %param.6) | copy-start | bytes 2949124
  2.5 0.8 copy-start.1
  3.4 0.8 copy-start.2

commit v5 on v4

--- a/solution.py
+++ b/solution.py
@@ -13,10 +13,10 @@
 HD = 128
 PAGE = 4
 REACH = 8
-GROUP = 3
+GROUPS = ((0, 4), (4, 3), (7, 2))
 COLUMNS = 4
 STOP = 8
-FORWARD = 12
+FORWARD = 13
 MESH = pl.DeviceIdType.MESH
 
 masked_score = -16384.0
@@ -24,13 +24,13 @@
 
 
 def ring_attention(
-    seq_count, q_ref, k_ref, v_ref, len_ref, owner_ref, slot_ref, o_ref, page_ref,
-    qs, held, bias, eye, ones, top, acc, total, send_sem, recv_sem,
+    seq_count, q_hbm, k_hbm, v_hbm, len_hbm, owner_hbm, slot_hbm, o_ref, page_ref,
+    len_ref, owner_ref, slot_ref, load_sem, qs, held, bias, eye, ones, top, acc, total, send_sem, recv_sem,
     picked, across, along, landed, tag_across, tag_along, tag_landed,
     stopped, tag_stopped,
     across_send, across_recv, along_send, along_recv, stop_send, stop_recv, from_right, from_left,
 ):
-    rows = k_ref.shape[0]
+    rows = k_hbm.shape[0]
     kv_local = held.shape[1]
     parts = 2 * kv_local
     mine = lax.axis_index("seq")
@@ -48,6 +48,28 @@
 
     def signal(sem, device):
         pl.semaphore_signal(sem, inc=1, device_id={"seq": device}, device_id_type=MESH)
+
+    own = pl.ds(0, rows)
+    pairs = [
+        (ref.at[:, pl.ds(c * HD, HD)], held.at[part, c, own])
+        for c in range(kv_local)
+        for part, ref in enumerate((k_hbm, v_hbm))
+    ]
+    pairs += [(owner_hbm, owner_ref), (slot_hbm, slot_ref), (len_hbm, len_ref)]
+    pairs += [
+        (
+            q_hbm.at[layer, :, pl.ds((c * QPER + i) * HD, HD)],
+            qs.at[c, layer, pl.ds(i * rows, rows)],
+        )
+        for c in range(kv_local)
+        for layer in range(LAYERS)
+        for i in range(QPER)
+    ]
+    loads = [
+        pltpu.make_async_copy(src, dst, load_sem.at[n]) for n, (src, dst) in enumerate(pairs)
+    ]
+    for load in loads:
+        load.start()
 
     barrier = pltpu.get_barrier_semaphore()
     signal(barrier, left)
@@ -56,16 +78,19 @@
     for offset in range(1, COLUMNS):
         signal(barrier, at_column(offset))
     pl.semaphore_wait(barrier, COLUMNS + 2)
-    signal(from_right, at_place(-1))
-    signal(from_left, at_place(1))
-
-    def hop(n, src=None):
+    def tell(level):
+        signal(from_right.at[level], at_place(-(1 << level)))
+        signal(from_left.at[level], at_place(1 << level))
+
+    def learn(level):
+        pl.semaphore_wait(from_right.at[level], 1)
+        pl.semaphore_wait(from_left.at[level], 1)
+
+    def hop(n):
         slot = n // parts
         c, part = (n % parts) // 2, n % 2
-        if src is None:
-            src = held.at[part, c, pl.ds(pl.multiple_of(slot * rows, rows), rows)]
         return pltpu.make_async_remote_copy(
-            src_ref=src,
+            src_ref=held.at[part, c, pl.ds(pl.multiple_of(slot * rows, rows), rows)],
             dst_ref=held.at[part, c, pl.ds(pl.multiple_of((slot + 1) * rows, rows), rows)],
             send_sem=send_sem.at[n],
             recv_sem=recv_sem.at[n],
@@ -74,7 +99,11 @@
         )
 
     for n in range(parts):
-        hop(n, (k_ref, v_ref)[n % 2].at[:, pl.ds((n // 2) * HD, HD)]).start()
+        loads[n].wait()
+        hop(n).start()
+    tell(0)
+    for load in loads[parts:parts + 3]:
+        load.wait()
 
     lines = places * PAGE
     unit = COLUMNS * PAGE
@@ -97,9 +126,7 @@
     goes = iota((seq_count * PAGE, kv_local * rows), 0).astype(jnp.float32) == owner_row * PAGE + line_row
     source = jnp.concatenate(
         [
-            jnp.concatenate(
-                [k_ref[:, c * HD:(c + 1) * HD], v_ref[:, c * HD:(c + 1) * HD]], axis=1
-            )
+            jnp.concatenate([held[0, c, own], held[1, c, own]], axis=1)
             for c in range(kv_local)
         ],
         axis=0,
@@ -165,13 +192,9 @@
             )
         ]
 
-    for c in range(kv_local):
-        held[0, c, pl.ds(0, rows)] = k_ref[:, c * HD:(c + 1) * HD]
-        held[1, c, pl.ds(0, rows)] = v_ref[:, c * HD:(c + 1) * HD]
-        for layer in range(LAYERS):
-            for i in range(QPER):
-                h = c * QPER + i
-                qs[c, layer, pl.ds(i * rows, rows)] = q_ref[layer, :, h * HD:(h + 1) * HD]
+    learn(0)
+    tell(1)
+
     reqs = len_ref.shape[1]
     lengths = len_ref[...].astype(jnp.float32)
     before = lax.broadcasted_iota(jnp.int32, (reqs, reqs), 1) < lax.broadcasted_iota(
@@ -192,11 +215,12 @@
     for i in range(QPER):
         eye[pl.ds(i * rows, rows)] = same.astype(jnp.bfloat16)
     ones[...] = jnp.ones_like(ones)
-    span = GROUP * rows
-
-    def piece(i, first, last=False):
+
+    def piece(i, group):
         c, layer = i // LAYERS, i % LAYERS
-        keys = pl.ds(first * rows, span)
+        first, count = GROUPS[group]
+        last = group == len(GROUPS) - 1
+        keys = pl.ds(first * rows, count * rows)
         wide_q = jnp.concatenate([qs[c, layer], eye[...]], axis=1)
         wide_k = jnp.concatenate([held[0, c, keys], bias[keys]], axis=1)
         scores = lax.dot_general(
@@ -209,7 +233,7 @@
             shrink = jnp.exp2((old - fresh) * exponent_scale)
             fresh = fresh[:, :1]
         weights = jnp.exp2((scores - fresh) * exponent_scale)
-        wide_v = jnp.concatenate([held[1, c, keys], ones[...]], axis=1)
+        wide_v = jnp.concatenate([held[1, c, keys], ones[pl.ds(0, count * rows)]], axis=1)
         product = jnp.dot(weights.astype(jnp.bfloat16), wide_v, preferred_element_type=jnp.float32)
         summed, counted = product[:, :HD], product[:, HD:]
         if first > 0:
@@ -245,15 +269,6 @@
     half = places // 2
     detour = half - FORWARD
 
-    def next_token(more):
-        pl.semaphore_wait(from_right, 1)
-        pl.semaphore_wait(from_left, 1)
-
-        @pl.when(more)
-        def _():
-            signal(from_right, at_place(-1))
-            signal(from_left, at_place(1))
-
     def send_both(k):
         for copy in to_place(-k, half + k):
             copy.start()
@@ -305,11 +320,9 @@
             )
         ]
 
-    def early(i):
-        next_token(i >= 0)
-        handle(i)
-
-    loop(STOP - 1, early)
+    learn(1)
+    tell(2)
+    loop(parts, handle)
     for offset in range(1, COLUMNS):
         for copy in to_column(offset):
             copy.wait_recv()
@@ -335,40 +348,45 @@
         tag_along[z] = tag_table[z:z + 1]
     landed[pl.ds(0, unit)] = along[pl.ds(pl.multiple_of(place * unit, unit), unit)]
     tag_landed[0] = tag_along[place]
+    learn(2)
+    tell(3)
     for j in range(detour):
         for copy in to_stop(j):
             copy.start()
     loop(STOP, lambda i: send_both(i + 1))
 
-    def late(i):
-        k = i + STOP + 1
-        next_token(k < half - 1)
-        handle(k - 2)
-        send_both(k)
-
-    loop(half - 1 - STOP, late)
+    loop(2 * parts, lambda i: handle(parts + i))
+    for load in loads[parts + 3:]:
+        load.wait()
+    learn(3)
+    loop(half - 1 - STOP, lambda i: send_both(STOP + 1 + i))
+    pieces = kv_local * LAYERS
+
+    def first_group(i):
+        handle(3 * parts + 2 * i)
+        piece(i, 0)
+        handle(3 * parts + 1 + 2 * i)
+
+    loop(pieces, first_group)
     for j in range(detour):
         for copy in to_stop(j):
             copy.wait_recv()
         for copy in from_stop(j):
             copy.start()
-    done_chunks = half - 2
-    pieces = kv_local * LAYERS
-
-    def first_group(i):
-        handle(done_chunks + i)
-        piece(i, 0)
-
-    loop(pieces, first_group)
+    next_chunk = 3 * parts + 2 * pieces
+    last_chunks = (REACH - 1) * parts
 
     def second_group(i):
-        handle(done_chunks + pieces + i)
-        piece(i, GROUP)
+        n = next_chunk + i
+        hop(n).wait_recv()
+
+        @pl.when(n < last_chunks)
+        def _():
+            hop(n + parts).start()
+
+        piece(i, 1)
 
     loop(pieces, second_group)
-    last_chunks = (REACH - 1) * parts
-    for n in range(done_chunks + 2 * pieces, last_chunks + 2):
-        handle(n, n < last_chunks)
 
     def wait_pages(i):
         for copy in to_place(1, i + 1):
@@ -392,11 +410,11 @@
     ).astype(page_ref.dtype)
 
     def third_group(i):
-        @pl.when(i < 2)
+        @pl.when(i < REACH * parts - next_chunk - pieces)
         def _():
-            handle(last_chunks + 2 + i, False)
-
-        piece(i, 2 * GROUP, True)
+            handle(next_chunk + pieces + i, False)
+
+        piece(i, 2)
 
     loop(pieces, third_group)
     loop(REACH * parts, lambda n: hop(n).wait_send())
@@ -432,14 +450,18 @@
             jax.ShapeDtypeStruct((LAYERS, rows, width), jnp.bfloat16),
             jax.ShapeDtypeStruct((slots * PAGE, 2 * HD), jnp.bfloat16),
         ),
-        in_specs=[pl.BlockSpec(memory_space=pltpu.VMEM)] * 6,
+        in_specs=[pl.BlockSpec(memory_space=pltpu.HBM)] * 6,
         out_specs=(pl.BlockSpec(memory_space=pltpu.VMEM), pl.BlockSpec(memory_space=pltpu.VMEM)),
         scratch_shapes=[
+            pltpu.VMEM((1, lengths.shape[0]), jnp.int32),
+            pltpu.VMEM((kv_local, pages_dev), jnp.int32),
+            pltpu.VMEM((kv_local, pages_dev), jnp.int32),
+            pltpu.SemaphoreType.DMA((2 * kv_local + 3 + kv_local * LAYERS * QPER,)),
             pltpu.VMEM((kv_local, LAYERS, wide, HD), jnp.bfloat16),
             pltpu.VMEM((2, kv_local, (REACH + 1) * rows, HD), jnp.bfloat16),
             pltpu.VMEM(((REACH + 1) * rows, rows), jnp.bfloat16),
             pltpu.VMEM((wide, rows), jnp.bfloat16),
-            pltpu.VMEM((GROUP * rows, HD), jnp.bfloat16),
+            pltpu.VMEM((max(count for _, count in GROUPS) * rows, HD), jnp.bfloat16),
             pltpu.VMEM((kv_local, LAYERS, wide, HD), jnp.float32),
             pltpu.VMEM((kv_local, LAYERS, wide, HD), jnp.float32),
             pltpu.VMEM((kv_local, LAYERS, wide, HD), jnp.float32),
@@ -460,15 +482,20 @@
             pltpu.SemaphoreType.DMA((2, places)),
             pltpu.SemaphoreType.DMA((2, detour)),
             pltpu.SemaphoreType.DMA((2, detour)),
-            pltpu.SemaphoreType.REGULAR,
-            pltpu.SemaphoreType.REGULAR,
+            pltpu.SemaphoreType.REGULAR((4,)),
+            pltpu.SemaphoreType.REGULAR((4,)),
         ],
         compiler_params=pltpu.CompilerParams(
             collective_id=0, has_side_effects=True, vmem_limit_bytes=28 * 1024 * 1024
         ),
     )(
-        queries.transpose(1, 0, 2), keys, values, lengths.reshape(1, -1),
-        page_owner.transpose(1, 0), page_slot.transpose(1, 0),
+        *(
+            pltpu.with_memory_space_constraint(x, pltpu.HBM)
+            for x in (
+                queries.transpose(1, 0, 2), keys, values, lengths.reshape(1, -1),
+                page_owner.transpose(1, 0), page_slot.transpose(1, 0),
+            )
+        )
     )
     return (attended.transpose(1, 0, 2), pages.reshape(slots, PAGE, 2 * HD))
 

time: 105 us -> 103 us (0.981)
  local copies, waits for them, and re-layouts: 5.19 us -> 1.64 us
    unnamed x13 -> x1, local copies, waits for them, and re-layouts: 4.5 us -> 0.94 us
where the time goes in v5:
time: 103 us; the launch traced here: 102 us
  Pallas kernels  100 us (97%)
  local copies, waits for them, and re-layouts  1.64 us (2%)
    pallas_call x1, Pallas kernels, shards(): pl.pallas_call(functools.partial(ring_attention, seq_count), name='ring_a...  100 us

profile of v5, /device:TPU:40, one launch (start us, length us, event | category | flops | bytes accessed | tf_op | source)
XLA Modules:
  0.0 102.5 jit_solution(12451548563755882640)
XLA Ops:
  0.6 100.2 %ring_attention.1 = (bf16[3,128,1280]{2,1,0:T(8,128)(2,1)S(1)}, bf16[256,256]{1,0:T(8,128)(2,1)S(1)}) custom-call(bf16[3,128,1280]{2,1,0:T(8,128)(2,1)} %bitcast.6, bf16[128,256]{1,0:T(8,128)(2,1)} %k_hbm.1, bf16[128,256]{1,0:T(8,128)(2,1)} %v_hbm.1, s32[1,64]{1,0:T(1,128)} %bitcast.9, s32[2,32]{1,0:T(2,128)} %bitcast.7, s32[2,32]{1,0:T(2,128)} %bitcast.8), custom_call_target="tpu_custom_call" | custom-call | tf_op jit(solution)/shard_map/ring_attention/pallas_call | solution.py:446
  100.8 0.7 reshape.11
  101.5 0.9 copy.9

commit v6 on v5

--- a/solution.py
+++ b/solution.py
@@ -13,10 +13,11 @@
 HD = 128
 PAGE = 4
 REACH = 8
-GROUPS = ((0, 4), (4, 3), (7, 2))
+GROUPS = ((0, 2), (2, 2), (4, 2), (6, 3))
 COLUMNS = 4
 STOP = 8
-FORWARD = 13
+FORWARD = 12
+NEAR = 4
 MESH = pl.DeviceIdType.MESH
 
 masked_score = -16384.0
@@ -192,9 +193,6 @@
             )
         ]
 
-    learn(0)
-    tell(1)
-
     reqs = len_ref.shape[1]
     lengths = len_ref[...].astype(jnp.float32)
     before = lax.broadcasted_iota(jnp.int32, (reqs, reqs), 1) < lax.broadcasted_iota(
@@ -215,6 +213,11 @@
     for i in range(QPER):
         eye[pl.ds(i * rows, rows)] = same.astype(jnp.bfloat16)
     ones[...] = jnp.ones_like(ones)
+    for offset in range(1, COLUMNS):
+        for copy in to_column(offset):
+            copy.start()
+    learn(0)
+    tell(1)
 
     def piece(i, group):
         c, layer = i // LAYERS, i % LAYERS
@@ -262,10 +265,6 @@
 
         lax.fori_loop(0, count, step, 0)
 
-    for offset in range(1, COLUMNS):
-        for copy in to_column(offset):
-            copy.start()
-
     half = places // 2
     detour = half - FORWARD
 
@@ -348,45 +347,51 @@
         tag_along[z] = tag_table[z:z + 1]
     landed[pl.ds(0, unit)] = along[pl.ds(pl.multiple_of(place * unit, unit), unit)]
     tag_landed[0] = tag_along[place]
+    loop(NEAR, lambda i: send_both(i + 1))
     learn(2)
     tell(3)
     for j in range(detour):
         for copy in to_stop(j):
             copy.start()
-    loop(STOP, lambda i: send_both(i + 1))
-
-    loop(2 * parts, lambda i: handle(parts + i))
+    loop(STOP - NEAR, lambda i: send_both(NEAR + 1 + i))
+
     for load in loads[parts + 3:]:
         load.wait()
+    pieces = kv_local * LAYERS
+    last_chunks = (REACH - 1) * parts
+
+    def beside(group):
+        first_chunk = (GROUPS[group][0] + 1) * parts
+
+        def step(i):
+            handle(first_chunk + i)
+            piece(i, group)
+
+        loop(pieces, step)
+        for n in range(first_chunk + pieces, first_chunk + 2 * parts):
+            handle(n)
+
+    beside(0)
     learn(3)
     loop(half - 1 - STOP, lambda i: send_both(STOP + 1 + i))
-    pieces = kv_local * LAYERS
-
-    def first_group(i):
-        handle(3 * parts + 2 * i)
-        piece(i, 0)
-        handle(3 * parts + 1 + 2 * i)
-
-    loop(pieces, first_group)
+    beside(1)
     for j in range(detour):
         for copy in to_stop(j):
             copy.wait_recv()
         for copy in from_stop(j):
             copy.start()
-    next_chunk = 3 * parts + 2 * pieces
-    last_chunks = (REACH - 1) * parts
-
-    def second_group(i):
-        n = next_chunk + i
-        hop(n).wait_recv()
-
-        @pl.when(n < last_chunks)
+    beside(2)
+    for n in range(last_chunks, last_chunks + 2):
+        handle(n, False)
+
+    def last_group(i):
+        @pl.when(i < 2)
         def _():
-            hop(n + parts).start()
-
-        piece(i, 1)
-
-    loop(pieces, second_group)
+            handle(last_chunks + 2 + i, False)
+
+        piece(i, 3)
+
+    loop(pieces, last_group)
 
     def wait_pages(i):
         for copy in to_place(1, i + 1):
@@ -409,14 +414,6 @@
         one_hot(put), landed[...], (((0,), (0,)), ((), ())), preferred_element_type=jnp.float32
     ).astype(page_ref.dtype)
 
-    def third_group(i):
-        @pl.when(i < REACH * parts - next_chunk - pieces)
-        def _():
-            handle(next_chunk + pieces + i, False)
-
-        piece(i, 2)
-
-    loop(pieces, third_group)
     loop(REACH * parts, lambda n: hop(n).wait_send())
     for offset in range(1, COLUMNS):
         for copy in to_column(offset):

time: 103 us -> 100 us (0.971)
  Pallas kernels: 100 us -> 97.6 us
    pallas_call x1, Pallas kernels: 100 us -> 97.6 us  [shards(): pl.pallas_call(functools.partial(ring_attention, seq_count), name='ring_a...]
where the time goes in v6:
time: 100 us; the launch traced here: 99.9 us
  Pallas kernels  97.6 us (98%)
  local copies, waits for them, and re-layouts  1.64 us (2%)
    pallas_call x1, Pallas kernels, shards(): pl.pallas_call(functools.partial(ring_attention, seq_count), name='ring_a...  97.6 us

profile of v6, /device:TPU:40, one launch (start us, length us, event | category | flops | bytes accessed | tf_op | source)
XLA Modules:
  0.0 99.9 jit_solution(3389996762702443840)
XLA Ops:
  0.6 97.6 %ring_attention.1 = (bf16[3,128,1280]{2,1,0:T(8,128)(2,1)S(1)}, bf16[256,256]{1,0:T(8,128)(2,1)S(1)}) custom-call(bf16[3,128,1280]{2,1,0:T(8,128)(2,1)} %bitcast.6, bf16[128,256]{1,0:T(8,128)(2,1)} %k_hbm.1, bf16[128,256]{1,0:T(8,128)(2,1)} %v_hbm.1, s32[1,64]{1,0:T(1,128)} %bitcast.9, s32[2,32]{1,0:T(2,128)} %bitcast.7, s32[2,32]{1,0:T(2,128)} %bitcast.8), custom_call_target="tpu_custom_call" | custom-call | tf_op jit(solution)/shard_map/ring_attention/pallas_call | solution.py:443
  98.3 0.7 reshape.11
  99.0 0.9 copy.9

commit v7 on v6

--- a/solution.py
+++ b/solution.py
@@ -268,14 +268,17 @@
     half = places // 2
     detour = half - FORWARD
 
-    def send_both(k):
+    def send_back(k):
         for copy in to_place(-k, half + k):
             copy.start()
 
-        @pl.when(k <= FORWARD)
-        def _():
-            for copy in to_place(k, k):
-                copy.start()
+    def send_ahead(k):
+        for copy in to_place(k, k):
+            copy.start()
+
+    def send_both(k):
+        send_back(k)
+        send_ahead(k)
 
     def to_stop(j):
         there = lax.rem(place + FORWARD + 1 + j, places)
@@ -373,14 +376,30 @@
 
     beside(0)
     learn(3)
-    loop(half - 1 - STOP, lambda i: send_both(STOP + 1 + i))
+    loop(half - 1 - STOP, lambda i: send_back(STOP + 1 + i))
     beside(1)
+    loop(FORWARD - STOP, lambda i: send_ahead(STOP + 1 + i))
     for j in range(detour):
         for copy in to_stop(j):
             copy.wait_recv()
         for copy in from_stop(j):
             copy.start()
     beside(2)
+
+    def wait_sent(landing):
+        for copy in to_place(1, landing):
+            copy.wait_send()
+
+    settled = 4 * parts
+    loop(settled + parts, lambda n: hop(n).wait_send())
+    for offset in range(1, COLUMNS):
+        for copy in to_column(offset):
+            copy.wait_send()
+    for j in range(detour):
+        for copy in to_stop(j):
+            copy.wait_send()
+    loop(STOP, lambda i: wait_sent(1 + i))
+    loop(STOP, lambda i: wait_sent(half + 1 + i))
     for n in range(last_chunks, last_chunks + 2):
         handle(n, False)
 
@@ -414,19 +433,9 @@
         one_hot(put), landed[...], (((0,), (0,)), ((), ())), preferred_element_type=jnp.float32
     ).astype(page_ref.dtype)
 
-    loop(REACH * parts, lambda n: hop(n).wait_send())
-    for offset in range(1, COLUMNS):
-        for copy in to_column(offset):
-            copy.wait_send()
-
-    def wait_sent(i):
-        for copy in to_place(1, i + 1):
-            copy.wait_send()
-
-    loop(places - 1, wait_sent)
-    for j in range(detour):
-        for copy in to_stop(j):
-            copy.wait_send()
+    loop(last_chunks - settled, lambda n: hop(settled + parts + n).wait_send())
+    loop(half - 1 - STOP, lambda i: wait_sent(half + STOP + 1 + i))
+    loop(half - STOP, lambda i: wait_sent(STOP + 1 + i))
 
 
 def shards(queries, keys, values, lengths, page_owner, page_slot):

time: 100 us -> 99.8 us (level)
  no operation moved by 1% of the time
where the time goes in v7:
time: 99.8 us; the launch traced here: 99.6 us
  Pallas kernels  97.4 us (98%)
  local copies, waits for them, and re-layouts  1.64 us (2%)
    pallas_call x1, Pallas kernels, shards(): pl.pallas_call(functools.partial(ring_attention, seq_count), name='ring_a...  97.4 us

profile of v7, /device:TPU:40, one launch (start us, length us, event | category | flops | bytes accessed | tf_op | source)
XLA Modules:
  0.0 99.6 jit_solution(9423797185096238950)
XLA Ops:
  0.6 97.4 %ring_attention.1 = (bf16[3,128,1280]{2,1,0:T(8,128)(2,1)S(1)}, bf16[256,256]{1,0:T(8,128)(2,1)S(1)}) custom-call(bf16[3,128,1280]{2,1,0:T(8,128)(2,1)} %bitcast.6, bf16[128,256]{1,0:T(8,128)(2,1)} %k_hbm.1, bf16[128,256]{1,0:T(8,128)(2,1)} %v_hbm.1, s32[1,64]{1,0:T(1,128)} %bitcast.9, s32[2,32]{1,0:T(2,128)} %bitcast.7, s32[2,32]{1,0:T(2,128)} %bitcast.8), custom_call_target="tpu_custom_call" | custom-call | tf_op jit(solution)/shard_map/ring_attention/pallas_call | solution.py:452
  98.0 0.7 reshape.11
  98.7 0.9 copy.9

commit v8 on v7

--- a/solution.py
+++ b/solution.py
@@ -18,6 +18,7 @@
 STOP = 8
 FORWARD = 12
 NEAR = 4
+LATEST = 10
 MESH = pl.DeviceIdType.MESH
 
 masked_score = -16384.0
@@ -363,7 +364,7 @@
     pieces = kv_local * LAYERS
     last_chunks = (REACH - 1) * parts
 
-    def beside(group):
+    def beside(group, then=None):
         first_chunk = (GROUPS[group][0] + 1) * parts
 
         def step(i):
@@ -371,6 +372,8 @@
             piece(i, group)
 
         loop(pieces, step)
+        if then is not None:
+            then()
         for n in range(first_chunk + pieces, first_chunk + 2 * parts):
             handle(n)
 
@@ -378,13 +381,13 @@
     learn(3)
     loop(half - 1 - STOP, lambda i: send_back(STOP + 1 + i))
     beside(1)
-    loop(FORWARD - STOP, lambda i: send_ahead(STOP + 1 + i))
+    loop(FORWARD - LATEST, lambda i: send_ahead(FORWARD - i))
     for j in range(detour):
         for copy in to_stop(j):
             copy.wait_recv()
         for copy in from_stop(j):
             copy.start()
-    beside(2)
+    beside(2, lambda: loop(LATEST - STOP, lambda i: send_ahead(LATEST - i)))
 
     def wait_sent(landing):
         for copy in to_place(1, landing):

time: 99.8 us -> 99 us (level)
  Pallas kernels: 97.4 us -> 95.6 us
    pallas_call x1, Pallas kernels: 97.4 us -> 95.6 us  [shards(): pl.pallas_call(functools.partial(ring_attention, seq_count), name='ring_a...]
where the time goes in v8:
time: 99 us; the launch traced here: 97.9 us
  Pallas kernels  95.6 us (97%)
  local copies, waits for them, and re-layouts  1.64 us (2%)
    pallas_call x1, Pallas kernels, shards(): pl.pallas_call(functools.partial(ring_attention, seq_count), name='ring_a...  95.6 us

profile of v8, /device:TPU:40, one launch (start us, length us, event | category | flops | bytes accessed | tf_op | source)
XLA Modules:
  0.0 97.9 jit_solution(5600406549257563594)
XLA Ops:
  0.6 95.6 %ring_attention.1 = (bf16[3,128,1280]{2,1,0:T(8,128)(2,1)S(1)}, bf16[256,256]{1,0:T(8,128)(2,1)S(1)}) custom-call(bf16[3,128,1280]{2,1,0:T(8,128)(2,1)} %bitcast.6, bf16[128,256]{1,0:T(8,128)(2,1)} %k_hbm.1, bf16[128,256]{1,0:T(8,128)(2,1)} %v_hbm.1, s32[1,64]{1,0:T(1,128)} %bitcast.9, s32[2,32]{1,0:T(2,128)} %bitcast.7, s32[2,32]{1,0:T(2,128)} %bitcast.8), custom_call_target="tpu_custom_call" | custom-call | tf_op jit(solution)/shard_map/ring_attention/pallas_call | solution.py:455
  96.2 0.7 reshape.11
  96.9 0.9 copy.9
